TPU v7x, 256 devices: a whole 4x4x8 slice. The times are simulated.
256 devices in a mesh: row: 32 (over x, y, core), col: 8 (over z).
Axes of the slice: x: 4, y: 4, z: 8, core: 2. Of those that a mesh axis runs over, the one named last changes fastest.
Arguments:
- matrix: float32 [5120, 5120], P('row', 'col'), may hold values from -64 to 64
Outputs:
- iterate: float32 [5120, 5120], P('row', 'col')
- trace_value: float32 [2], replicated
- frobenius: float32 [2], replicated
All inputs are finite; a program needn't handle non-finite values.
Results may differ from a plain program's by a relative error of at most 0.003.
Values may be sent and summed in bfloat16 or wider, within the bound.
No kernel may reach another device: no remote copies, remote signals or barrier semaphores. Data moves between devices by JAX's collectives and lax.ppermute only.
A program may use at most 64 MiB of HBM per device.

v0:
```python
import functools
import jax
import jax.numpy as jnp
import numpy as np
from jax import lax
from jax.experimental import pallas as pl
from jax.experimental.pallas import tpu as pltpu
from jax.sharding import Mesh
from jax.sharding import PartitionSpec as P

NX, NY, NC, NZ = 4, 4, 2, 8
AXES = ("x", "y", "c", "z")
TARGET = 0.0625

EVERY = [
    (x, y, c, z) for x in range(NX) for y in range(NY) for c in range(NC) for z in range(NZ)
]


def rank(x, y, c, z):
    return ((x * NY + y) * NC + c) * NZ + z


def even_pair(i, n):
    return i ^ 1


def odd_pair(i, n):
    return (((i - 1) % n ^ 1) + 1) % n


PAIRS = (even_pair, odd_pair)


def permute(value, target):
    return lax.ppermute(value, AXES, [(rank(*d), rank(*target(*d))) for d in EVERY])


def along_z(turn):
    return lambda x, y, c, z: (x, y, 1 - c, PAIRS[turn ^ c ^ (z & 1)](z, NZ))


def along_xy(second, turn):
    def target(x, y, c, z):
        if second ^ c ^ ((x + y) & 1):
            return (x, PAIRS[turn](y, NY), 1 - c, z)
        return (PAIRS[turn](x, NX), y, 1 - c, z)

    return target


def join(*parts):
    return jnp.concatenate(parts, axis=0)


def z_order(group, z):
    a, b = PAIRS[group], PAIRS[1 - group]
    two = lambda i: [i, a(i, NZ)]
    third = b(a(z, NZ), NZ)
    fourth = b(a(b(z, NZ), NZ), NZ)
    return two(z) + two(b(z, NZ)) + two(third) + two(fourth)


def xy_places(x, y, group, half, flip):
    a, b = PAIRS[half], PAIRS[1 - half]
    i, j = (x, y) if group == 0 else (y, x)
    four = lambda k: [k, a(k, 4), b(k, 4), a(b(k, 4), 4)]
    places = []
    for jj in four(j):
        for ii in four(i):
            xx, yy = (ii, jj) if group == 0 else (jj, ii)
            core = group ^ ((xx + yy) & 1) ^ flip
            places.append(((xx * NY + yy) * NC + core) * 2 + half)
    return places


def xy_order(x, y, c, flip):
    group = c ^ ((x + y) & 1)
    own = [xy_places(x, y, group, half, flip) for half in range(2)]
    other = [xy_places(x, y, 1 - group, half, flip) for half in range(2)]
    return own[0] + own[1] + other[0][:8] + other[1][:8] + other[0][8:] + other[1][8:]


XY_COUNT = 4 * NX * NY


def order_table():
    lines = [
        xy_order(x, y, c, 0) + xy_order(x, y, c, z & 1) + z_order(c ^ (z & 1), z)
        for (x, y, c, z) in EVERY
    ]
    return np.array(lines, dtype=np.int32)


def vmem():
    return pl.BlockSpec(memory_space=pltpu.VMEM)


def smem():
    return pl.BlockSpec(memory_space=pltpu.SMEM)


def fold_rows(values):
    rows, cols = values.shape
    return jnp.sum(values.reshape(rows // 8, 8, cols), axis=0)


def fold_lanes(values):
    total = values[:, :128]
    for k in range(128, values.shape[1], 128):
        total = total + values[:, k : k + 128]
    return total


def fold(values):
    return fold_lanes(fold_rows(values))


EXTRA = 16


def write_parts(values, out, first):
    rest = values
    for k in range(3):
        part = rest.astype(jnp.bfloat16)
        rest = rest - part.astype(jnp.float32)
        block = jnp.concatenate([part, jnp.zeros_like(part)], axis=0)
        out[first : first + EXTRA, k * 128 : (k + 1) * 128] = block
    width = out.shape[1] - 384
    out[first : first + EXTRA, 384:] = jnp.zeros((EXTRA, width), jnp.bfloat16)


def read_parts(piece, first):
    total = jnp.zeros((8, 128), jnp.float32)
    for k in range(3):
        block = piece[first : first + EXTRA, k * 128 : (k + 1) * 128]
        total = total + block.astype(jnp.float32)[:8, :]
    return total


def prepare_body(matrix, tile, top, bottom):
    half = tile.shape[0] // 2
    rounded = matrix[...].astype(jnp.bfloat16)
    tile[...] = rounded
    top[...] = rounded[:half]
    bottom[...] = rounded[half:]


def prepare(matrix):
    rows, cols = matrix.shape
    shapes = [(rows, cols), (rows // 2, cols), (rows // 2, cols)]
    return pl.pallas_call(
        prepare_body,
        out_shape=[jax.ShapeDtypeStruct(s, jnp.bfloat16) for s in shapes],
        in_specs=[vmem()],
        out_specs=[vmem()] * 3,
        name="prepare",
        compiler_params=pltpu.CompilerParams(vmem_limit_bytes=4 * 2**20),
    )(matrix)


def lay_rows(order, pieces, wide, first, rows):
    cols = pieces[0].shape[1]
    stride = pieces[0].shape[0] // 2
    spot = 2 * XY_COUNT
    for piece in pieces:
        for k in range(piece.shape[0] // stride):
            start = pl.multiple_of(order[spot] * cols, 128)
            wide[first : first + rows, pl.ds(start, cols)] = piece[k * stride : k * stride + rows, :]
            spot += 1


def multiply(wide, panel, total):
    block = 2 * total.shape[1]

    def add(k, carry):
        start = pl.multiple_of(k * block, block)
        part = jnp.dot(
            wide[:, pl.ds(start, block)],
            panel[pl.ds(start, block), :],
            preferred_element_type=jnp.float32,
        )
        total[...] += part
        return carry

    total[...] = jnp.zeros(total.shape, jnp.float32)
    lax.fori_loop(0, wide.shape[1] // block, add, 0)


def first_body(step, n_right, n_left, order, *refs):
    right = refs[:n_right]
    left = refs[n_right : n_right + n_left]
    top, bottom, panel, wide, summed = refs[n_right + n_left :]
    rows, cols = summed.shape
    half = rows // 2
    spot = step * XY_COUNT
    for piece in right:
        count = piece.shape[0] // half

        def place(k, carry, piece=piece, spot=spot):
            source = pl.multiple_of(k * half, half)
            start = pl.multiple_of(order[spot + k] * half, half)
            panel[pl.ds(start, half), :] = piece[pl.ds(source, half), :]
            return carry

        lax.fori_loop(0, count, place, 0)
        spot += count
    lay_rows(order, left, wide, 0, rows)
    multiply(wide, panel, summed)
    top[:half, :] = summed[:half, :].astype(jnp.bfloat16)
    bottom[...] = summed[half:, :].astype(jnp.bfloat16)
    if step == 0:
        block = 128

        def add(k, total):
            start = pl.multiple_of(k * block, block)
            part = panel[pl.ds(start, block), :].astype(jnp.float32)
            return total + fold_rows(part * part)

        total = jnp.zeros((8, cols), jnp.float32)
        total = lax.fori_loop(0, panel.shape[0] // block, add, total)
        write_parts(fold_lanes(total), top, half)


def first_product(step, order, right, left, rows, cols):
    full = cols * NZ
    half = rows // 2
    extra = EXTRA if step == 0 else 0
    shapes = [
        jax.ShapeDtypeStruct((half + extra, cols), jnp.bfloat16),
        jax.ShapeDtypeStruct((half, cols), jnp.bfloat16),
        jax.ShapeDtypeStruct((full, cols), jnp.bfloat16),
    ]
    return pl.pallas_call(
        functools.partial(first_body, step, len(right), len(left)),
        out_shape=shapes,
        in_specs=[smem()] + [vmem()] * (len(right) + len(left)),
        out_specs=[vmem()] * len(shapes),
        scratch_shapes=[
            pltpu.VMEM((rows, full), jnp.bfloat16),
            pltpu.VMEM((rows, cols), jnp.float32),
        ],
        name="first_product",
        compiler_params=pltpu.CompilerParams(vmem_limit_bytes=14 * 2**20),
        cost_estimate=pl.CostEstimate(
            flops=2 * rows * cols * full, bytes_accessed=2 * full * cols, transcendentals=0
        ),
    )(order, *right, *left)


def second_body(last, n_left, order, shift, panel, current, *refs):
    left = refs[:n_left]
    outs = refs[n_left:]
    if last:
        earlier, outs = outs[0], outs[1:]
    wide, summed = outs[-2], outs[-1]
    rows, cols = current.shape
    half = rows // 2
    lay_rows(order, left[: n_left // 2], wide, 0, half)
    lay_rows(order, left[n_left // 2 :], wide, half, half)
    multiply(wide, panel, summed)
    value = 1.5 * current[...].astype(jnp.float32)
    if last:
        value = value - 0.5 * summed[...]
    else:
        partial = jnp.zeros((8, 128), jnp.float32)
        for piece in left[: n_left // 2]:
            for k in range(2):
                partial = partial + read_parts(piece, k * (half + EXTRA) + half)
        squares = jnp.sum(jnp.sum(partial, axis=0, keepdims=True), axis=1, keepdims=True)
        scale = TARGET * (cols * NZ) / (squares + 1e-06)
        value = jnp.sqrt(scale) * (value - 0.5 * (scale * summed[...]))
    outs[0][...] = value
    r = lax.broadcasted_iota(jnp.int32, (rows, cols), 0)
    k = lax.broadcasted_iota(jnp.int32, (rows, cols), 1)
    diagonal = fold(jnp.where(k - r == shift[0], value, 0.0))
    power = fold(value * value)
    stats = outs[1]
    if last:
        stats[:16, :] = earlier[...]
        stats[16:24, :] = diagonal
        stats[24:, :] = power
    else:
        stats[:8, :] = diagonal
        stats[8:, :] = power
        rounded = value.astype(jnp.bfloat16)
        outs[2][...] = rounded
        outs[3][...] = rounded[: rows // 2]
        outs[4][...] = rounded[rows // 2 :]


def second_product(order, shift, panel, current, left, earlier):
    last = earlier is not None
    more = [earlier] if last else []
    rows, cols = current.shape
    full = cols * NZ
    shapes = [
        jax.ShapeDtypeStruct((rows, cols), jnp.float32),
        jax.ShapeDtypeStruct((32 if last else 16, 128), jnp.float32),
    ]
    if not last:
        shapes.append(jax.ShapeDtypeStruct((rows, cols), jnp.bfloat16))
        shapes += [jax.ShapeDtypeStruct((rows // 2, cols), jnp.bfloat16)] * 2
    return pl.pallas_call(
        functools.partial(second_body, last, len(left)),
        out_shape=shapes,
        in_specs=[smem()] * 2 + [vmem()] * (2 + len(left) + len(more)),
        out_specs=[vmem()] * len(shapes),
        scratch_shapes=[
            pltpu.VMEM((rows, full), jnp.bfloat16),
            pltpu.VMEM((rows, cols), jnp.float32),
        ],
        name="second_product",
        compiler_params=pltpu.CompilerParams(vmem_limit_bytes=14 * 2**20),
        cost_estimate=pl.CostEstimate(
            flops=2 * rows * cols * full, bytes_accessed=2 * full * cols, transcendentals=0
        ),
    )(order, shift, panel, current, *left, *more)


def in_step(*values):
    return lax.optimization_barrier(values)


def to_sibling(x, y, c, z):
    return (x, y, 1 - c, z)


def panels(tile, top, bottom):
    left = []
    right = []
    piece = tile
    for turn in range(4):
        moved = permute(piece, along_z(turn % 2))
        piece = join(piece, moved) if turn == 0 else moved
        left.append(piece)
    for half, part in enumerate((top, bottom)):
        for turn in range(4):
            moved = permute(part, along_xy(turn // 2, (turn + half) % 2))
            if turn < 3:
                part = join(part, moved)
        right += [part, moved]
    first = permute(join(right[0], right[2]), to_sibling)
    second = permute(join(right[1], right[3]), to_sibling)
    return right + [first, second], left


def row_panel(top, bottom):
    left = []
    for part in (top, bottom):
        piece = part
        for turn in range(4):
            moved = permute(piece, along_z(turn % 2))
            piece = join(piece, moved) if turn == 0 else moved
            left.append(piece)
    return left


def row_target(second, turn):
    def target(x, y, c, z):
        if second:
            return (x, PAIRS[turn](y, NY), 1 - c, z)
        return (PAIRS[turn](x, NX), y, 1 - c, z)

    return target


def totals(stats):
    stats = stats + permute(stats, to_sibling)
    for k in range(4):
        stats = stats + permute(stats, row_target(k // 2, k % 2))
    for step in (1, 2, 4):
        stats = stats + permute(stats, lambda x, y, c, z: (x, y, 1 - c, z ^ step))
    return jnp.sum(stats.reshape(2, 2, 8, 128), axis=(2, 3))


def on_device(matrix):
    rows, cols = matrix.shape
    me = lax.axis_index(AXES)
    z = lax.axis_index("z")
    moved_row = z % 2 == 1
    order = lax.dynamic_index_in_dim(jnp.asarray(order_table()), me, 0, keepdims=False)
    core = jnp.bitwise_xor(lax.axis_index("c"), z % 2)
    row_first = (lax.axis_index(("x", "y")) * NC + core) * rows
    shift = (row_first - z * cols).reshape(1)
    order, shift, matrix = in_step(order, shift, matrix)
    tile, top, bottom = prepare(matrix)

    tile = jnp.where(moved_row, permute(tile, to_sibling), tile)
    right, left = panels(tile, top, bottom)
    s_top, s_bottom, panel = first_product(0, order, right, left, rows, cols)
    left = row_panel(s_top, s_bottom)
    current, stats, tile, top, bottom = second_product(order, shift, panel, tile, left, None)
    right, left = panels(tile, top, bottom)
    s_top, s_bottom, panel = first_product(1, order, right, left, rows, cols)
    left = row_panel(s_top, s_bottom)
    current, stats = second_product(order, shift, panel, current, left, stats)
    current = jnp.where(moved_row, permute(current, to_sibling), current)
    sums = totals(stats)
    return (current, sums[:, 0], jnp.sqrt(sums[:, 1]))


def solution(mesh):
    split = Mesh(mesh.devices.reshape(NX, NY, NC, NZ), AXES)
    return jax.shard_map(
        on_device,
        mesh=split,
        in_specs=(P(("x", "y", "c"), "z"),),
        out_specs=(P(("x", "y", "c"), "z"), P(), P()),
        check_vma=False,
    )
```

profile of v0, /device:TPU:32, one launch (start us, length us, event | category | flops | bytes accessed | tf_op | source)
XLA Modules:
  0.0 238.0 jit_solution(5527654689853811944)
XLA Ops:
  9.5 3.6 %collective-permute-done.1 = bf16[160,640]{1,0:T(8,128)(2,1)S(1)} collective-permute-done((bf16[160,640]{1,0:T(8,128)(2,1)S(1)}, bf16[160,640]{1,0:T(8,128)(2,1)S(1)}, u32[]{:S(2)}, u32[]{:S(2)}) %collective-permute-start.1) | collective-permute-done | bytes 204832 | tf_op jit(solution)/shard_map/ppermute | solution.py:36
  27.0 8.3 %collective-permute-done.7.refs_3_ = bf16[640,640]{1,0:T(8,128)(2,1)S(1)} collective-permute-done((bf16[640,640]{1,0:T(8,128)(2,1)S(1)}, bf16[640,640]{1,0:T(8,128)(2,1)S(1)}, u32[]{:S(2)}, u32[]{:S(2)}) %collective-permute-start.7) | collective-permute-done | bytes 819232 | tf_op jit(solution)/shard_map/ppermute | solution.py:36
  39.5 4.4 %collective-permute-done.11 = bf16[160,640]{1,0:T(8,128)(2,1)S(1)} collective-permute-done((bf16[160,640]{1,0:T(8,128)(2,1)S(1)}, bf16[160,640]{1,0:T(8,128)(2,1)S(1)}, u32[]{:S(2)}, u32[]{:S(2)}) %collective-permute-start.11) | collective-permute-done | bytes 204832 | tf_op jit(solution)/shard_map/ppermute | solution.py:36
  43.9 4.0 %collective-permute-start.12 = (bf16[320,640]{1,0:T(8,128)(2,1)S(1)}, bf16[320,640]{1,0:T(8,128)(2,1)S(1)}, u32[]{:S(2)}, u32[]{:S(2)}) collective-permute-start(bf16[320,640]{1,0:T(8,128)(2,1)S(1)} %pad_maximum_fusion.4.refs_6_), channel_id=1, source_target_pairs={{0,15},{1,8},{2,9},{3,10},{4,11},{5,12},{6,13},{7,14},{8,1},{9,2},... | collective-permute-start | bytes 1228808 | tf_op jit(solution)/shard_map/ppermute | solution.py:36
  47.9 5.6 %collective-permute-done.12.refs_7_ = bf16[320,640]{1,0:T(8,128)(2,1)S(1)} collective-permute-done((bf16[320,640]{1,0:T(8,128)(2,1)S(1)}, bf16[320,640]{1,0:T(8,128)(2,1)S(1)}, u32[]{:S(2)}, u32[]{:S(2)}) %collective-permute-start.12) | collective-permute-done | bytes 409632 | tf_op jit(solution)/shard_map/ppermute | solution.py:36
  54.4 6.6 %collective-permute-done.13.refs_8_ = bf16[320,640]{1,0:T(8,128)(2,1)S(1)} collective-permute-done((bf16[320,640]{1,0:T(8,128)(2,1)S(1)}, bf16[320,640]{1,0:T(8,128)(2,1)S(1)}, u32[]{:S(2)}, u32[]{:S(2)}) %collective-permute-start.13) | collective-permute-done | bytes 409632 | tf_op jit(solution)/shard_map/ppermute | solution.py:36
  60.9 3.1 %collective-permute-start.14 = (bf16[320,640]{1,0:T(8,128)(2,1)S(1)}, bf16[320,640]{1,0:T(8,128)(2,1)S(1)}, u32[]{:S(2)}, u32[]{:S(2)}) collective-permute-start(bf16[320,640]{1,0:T(8,128)(2,1)S(1)} %collective-permute-done.13.refs_8_), channel_id=1, source_target_pairs={{0,15},{1,8},{2,9},{3,10},{4,11},{5,12},{6,13},{7,14},{8,1},{9,2},... | collective-permute-start | bytes 1228808 | tf_op jit(solution)/shard_map/ppermute | solution.py:36
  64.0 5.6 %collective-permute-done.14.refs_9_ = bf16[320,640]{1,0:T(8,128)(2,1)S(1)} collective-permute-done((bf16[320,640]{1,0:T(8,128)(2,1)S(1)}, bf16[320,640]{1,0:T(8,128)(2,1)S(1)}, u32[]{:S(2)}, u32[]{:S(2)}) %collective-permute-start.14) | collective-permute-done | bytes 409632 | tf_op jit(solution)/shard_map/ppermute | solution.py:36
  69.6 4.6 %first_product.2 = (bf16[96,640]{1,0:T(8,128)(2,1)S(1)}, bf16[80,640]{1,0:T(8,128)(2,1)S(1)}, bf16[5120,640]{1,0:T(8,128)(2,1)S(1)}) custom-call(s32[136]{0:T(256)S(1)} %bitcast.2, bf16[640,640]{1,0:T(8,128)(2,1)S(1)} %get-tuple-element.50.refs_0_, bf16[640,640]{1,0:T(8,128)(2,1)S(1)} %collective-permute-done.3.refs_1_, ...), custom_call_target="tpu_custom_call" | custom-call | flops 1048576000 | bytes 6553600 | tf_op jit(solution)/shard_map/first_product/pallas_call | solution.py:234
  78.6 3.3 %collective-permute-start.16 = (bf16[192,640]{1,0:T(8,128)(2,1)S(1)}, bf16[192,640]{1,0:T(8,128)(2,1)S(1)}, u32[]{:S(2)}, u32[]{:S(2)}) collective-permute-start(bf16[192,640]{1,0:T(8,128)(2,1)S(1)} %constant_dynamic-update-slice_fusion.16.refs_0_), channel_id=1, source_target_pairs={{0,15},{1,8},{2,9},{3,10},{4,11},{5,12},{6,13},{7,14},{8,1},{9,2},... | collective-permute-start | bytes 737288 | tf_op jit(solution)/shard_map/ppermute | solution.py:36
  88.5 3.0 %collective-permute-done.17.refs_2_ = bf16[192,640]{1,0:T(8,128)(2,1)S(1)} collective-permute-done((bf16[192,640]{1,0:T(8,128)(2,1)S(1)}, bf16[192,640]{1,0:T(8,128)(2,1)S(1)}, u32[]{:S(2)}, u32[]{:S(2)}) %collective-permute-start.17) | collective-permute-done | bytes 245792 | tf_op jit(solution)/shard_map/ppermute | solution.py:36
  91.5 3.2 %collective-permute-start.18 = (bf16[192,640]{1,0:T(8,128)(2,1)S(1)}, bf16[192,640]{1,0:T(8,128)(2,1)S(1)}, u32[]{:S(2)}, u32[]{:S(2)}) collective-permute-start(bf16[192,640]{1,0:T(8,128)(2,1)S(1)} %collective-permute-done.17.refs_2_), channel_id=1, source_target_pairs={{0,15},{1,8},{2,9},{3,10},{4,11},{5,12},{6,13},{7,14},{8,1},{9,2},... | collective-permute-start | bytes 737288 | tf_op jit(solution)/shard_map/ppermute | solution.py:36
  96.9 3.9 %collective-permute-done.22.refs_7_ = bf16[160,640]{1,0:T(8,128)(2,1)S(1)} collective-permute-done((bf16[160,640]{1,0:T(8,128)(2,1)S(1)}, bf16[160,640]{1,0:T(8,128)(2,1)S(1)}, u32[]{:S(2)}, u32[]{:S(2)}) %collective-permute-start.22) | collective-permute-done | bytes 204832 | tf_op jit(solution)/shard_map/ppermute | solution.py:36
  100.8 3.1 %second_product.2 = (f32[160,640]{1,0:T(8,128)S(1)}, f32[16,128]{1,0:T(8,128)S(1)}, bf16[160,640]{1,0:T(8,128)(2,1)S(1)}, bf16[80,640]{1,0:T(8,128)(2,1)S(1)}, bf16[80,640]{1,0:T(8,128)(2,1)S(1)}) custom-call(s32[136]{0:T(256)S(1)} %bitcast.3, s32[1]{0:T(128)} %bitcast.1.shift, bf16[5120,640]{1,0:T(8,128)(2,1)S(1)} %get-tuple-element.28.panel, ...), custom_call_target="tpu_custom_call" | custom-call | flops 1048576000 | bytes 6553600 | tf_op jit(solution)/shard_map/second_product/pallas_call | solution.py:304
  110.5 4.1 %collective-permute-done.24 = bf16[160,640]{1,0:T(8,128)(2,1)S(1)} collective-permute-done((bf16[160,640]{1,0:T(8,128)(2,1)S(1)}, bf16[160,640]{1,0:T(8,128)(2,1)S(1)}, u32[]{:S(2)}, u32[]{:S(2)}) %collective-permute-start.24) | collective-permute-done | bytes 204832 | tf_op jit(solution)/shard_map/ppermute | solution.py:36
  117.8 4.2 %collective-permute-done.25 = bf16[320,640]{1,0:T(8,128)(2,1)S(1)} collective-permute-done((bf16[320,640]{1,0:T(8,128)(2,1)S(1)}, bf16[320,640]{1,0:T(8,128)(2,1)S(1)}, u32[]{:S(2)}, u32[]{:S(2)}) %collective-permute-start.25) | collective-permute-done | bytes 409632 | tf_op jit(solution)/shard_map/ppermute | solution.py:36
  126.8 9.5 %collective-permute-done.30.refs_3_ = bf16[640,640]{1,0:T(8,128)(2,1)S(1)} collective-permute-done((bf16[640,640]{1,0:T(8,128)(2,1)S(1)}, bf16[640,640]{1,0:T(8,128)(2,1)S(1)}, u32[]{:S(2)}, u32[]{:S(2)}) %collective-permute-start.30) | collective-permute-done | bytes 819232 | tf_op jit(solution)/shard_map/ppermute | solution.py:36
  138.6 4.8 %collective-permute-done.33 = bf16[160,640]{1,0:T(8,128)(2,1)S(1)} collective-permute-done((bf16[160,640]{1,0:T(8,128)(2,1)S(1)}, bf16[160,640]{1,0:T(8,128)(2,1)S(1)}, u32[]{:S(2)}, u32[]{:S(2)}) %collective-permute-start.33) | collective-permute-done | bytes 204832 | tf_op jit(solution)/shard_map/ppermute | solution.py:36
  143.5 3.7 %collective-permute-start.34 = (bf16[320,640]{1,0:T(8,128)(2,1)S(1)}, bf16[320,640]{1,0:T(8,128)(2,1)S(1)}, u32[]{:S(2)}, u32[]{:S(2)}) collective-permute-start(bf16[320,640]{1,0:T(8,128)(2,1)S(1)} %constant_dynamic-update-slice_fusion.36.refs_6_), channel_id=1, source_target_pairs={{0,15},{1,8},{2,9},{3,10},{4,11},{5,12},{6,13},{7,14},{8,1},{9,2},... | collective-permute-start | bytes 1228808 | tf_op jit(solution)/shard_map/ppermute | solution.py:36
  147.2 5.6 %collective-permute-done.34.refs_7_ = bf16[320,640]{1,0:T(8,128)(2,1)S(1)} collective-permute-done((bf16[320,640]{1,0:T(8,128)(2,1)S(1)}, bf16[320,640]{1,0:T(8,128)(2,1)S(1)}, u32[]{:S(2)}, u32[]{:S(2)}) %collective-permute-start.34) | collective-permute-done | bytes 409632 | tf_op jit(solution)/shard_map/ppermute | solution.py:36
  153.6 6.6 %collective-permute-done.35.refs_8_ = bf16[320,640]{1,0:T(8,128)(2,1)S(1)} collective-permute-done((bf16[320,640]{1,0:T(8,128)(2,1)S(1)}, bf16[320,640]{1,0:T(8,128)(2,1)S(1)}, u32[]{:S(2)}, u32[]{:S(2)}) %collective-permute-start.35) | collective-permute-done | bytes 409632 | tf_op jit(solution)/shard_map/ppermute | solution.py:36
  160.2 3.2 %collective-permute-start.36 = (bf16[320,640]{1,0:T(8,128)(2,1)S(1)}, bf16[320,640]{1,0:T(8,128)(2,1)S(1)}, u32[]{:S(2)}, u32[]{:S(2)}) collective-permute-start(bf16[320,640]{1,0:T(8,128)(2,1)S(1)} %collective-permute-done.35.refs_8_), channel_id=1, source_target_pairs={{0,15},{1,8},{2,9},{3,10},{4,11},{5,12},{6,13},{7,14},{8,1},{9,2},... | collective-permute-start | bytes 1228808 | tf_op jit(solution)/shard_map/ppermute | solution.py:36
  163.4 5.6 %collective-permute-done.36.refs_9_ = bf16[320,640]{1,0:T(8,128)(2,1)S(1)} collective-permute-done((bf16[320,640]{1,0:T(8,128)(2,1)S(1)}, bf16[320,640]{1,0:T(8,128)(2,1)S(1)}, u32[]{:S(2)}, u32[]{:S(2)}) %collective-permute-start.36) | collective-permute-done | bytes 409632 | tf_op jit(solution)/shard_map/ppermute | solution.py:36
  169.1 3.7 %first_product.3 = (bf16[80,640]{1,0:T(8,128)(2,1)S(1)}, bf16[80,640]{1,0:T(8,128)(2,1)S(1)}, bf16[5120,640]{1,0:T(8,128)(2,1)S(1)}) custom-call(s32[136]{0:T(256)S(1)} %bitcast.4, bf16[640,640]{1,0:T(8,128)(2,1)S(1)} %get-tuple-element.46.refs_0_, bf16[640,640]{1,0:T(8,128)(2,1)S(1)} %collective-permute-done.26.refs_1_, ...), custom_call_target="tpu_custom_call" | custom-call | flops 1048576000 | bytes 6553600 | tf_op jit(solution)/shard_map/first_product/pallas_call | solution.py:234
  174.7 3.3 %collective-permute-done.41 = bf16[80,640]{1,0:T(8,128)(2,1)S(1)} collective-permute-done((bf16[80,640]{1,0:T(8,128)(2,1)S(1)}, bf16[80,640]{1,0:T(8,128)(2,1)S(1)}, u32[]{:S(2)}, u32[]{:S(2)}) %collective-permute-start.41) | collective-permute-done | bytes 102432 | tf_op jit(solution)/shard_map/ppermute | solution.py:36
  178.1 4.7 %collective-permute-start.42 = (bf16[160,640]{1,0:T(8,128)(2,1)S(1)}, bf16[160,640]{1,0:T(8,128)(2,1)S(1)}, u32[]{:S(2)}, u32[]{:S(2)}) collective-permute-start(bf16[160,640]{1,0:T(8,128)(2,1)S(1)} %constant_dynamic-update-slice_fusion.40.refs_4_), channel_id=1, source_target_pairs={{0,15},{1,8},{2,9},{3,10},{4,11},{5,12},{6,13},{7,14},{8,1},{9,2},... | collective-permute-start | bytes 614408 | tf_op jit(solution)/shard_map/ppermute | solution.py:36
  182.9 3.3 %collective-permute-done.42.refs_5_ = bf16[160,640]{1,0:T(8,128)(2,1)S(1)} collective-permute-done((bf16[160,640]{1,0:T(8,128)(2,1)S(1)}, bf16[160,640]{1,0:T(8,128)(2,1)S(1)}, u32[]{:S(2)}, u32[]{:S(2)}) %collective-permute-start.42) | collective-permute-done | bytes 204832 | tf_op jit(solution)/shard_map/ppermute | solution.py:36
  191.4 3.2 %collective-permute-start.44 = (bf16[160,640]{1,0:T(8,128)(2,1)S(1)}, bf16[160,640]{1,0:T(8,128)(2,1)S(1)}, u32[]{:S(2)}, u32[]{:S(2)}) collective-permute-start(bf16[160,640]{1,0:T(8,128)(2,1)S(1)} %collective-permute-done.43.refs_6_), channel_id=1, source_target_pairs={{0,15},{1,8},{2,9},{3,10},{4,11},{5,12},{6,13},{7,14},{8,1},{9,2},... | collective-permute-start | bytes 614408 | tf_op jit(solution)/shard_map/ppermute | solution.py:36
  194.6 3.9 %collective-permute-start.40 = (bf16[160,640]{1,0:T(8,128)(2,1)S(1)}, bf16[160,640]{1,0:T(8,128)(2,1)S(1)}, u32[]{:S(2)}, u32[]{:S(2)}) collective-permute-start(bf16[160,640]{1,0:T(8,128)(2,1)S(1)} %collective-permute-done.39.refs_2_), channel_id=1, source_target_pairs={{0,15},{1,8},{2,9},{3,10},{4,11},{5,12},{6,13},{7,14},{8,1},{9,2},... | collective-permute-start | bytes 614408 | tf_op jit(solution)/shard_map/ppermute | solution.py:36
  198.5 3.4 %collective-permute-done.40.refs_3_ = bf16[160,640]{1,0:T(8,128)(2,1)S(1)} collective-permute-done((bf16[160,640]{1,0:T(8,128)(2,1)S(1)}, bf16[160,640]{1,0:T(8,128)(2,1)S(1)}, u32[]{:S(2)}, u32[]{:S(2)}) %collective-permute-start.40) | collective-permute-done | bytes 204832 | tf_op jit(solution)/shard_map/ppermute | solution.py:36
  224.9 4.1 %collective-permute-done.52 = f32[32,128]{1,0:T(8,128)S(1)} collective-permute-done((f32[32,128]{1,0:T(8,128)S(1)}, f32[32,128]{1,0:T(8,128)S(1)}, u32[]{:S(2)}, u32[]{:S(2)}) %collective-permute-start.52) | collective-permute-done | bytes 16416 | tf_op jit(solution)/shard_map/ppermute | solution.py:36
  230.1 6.1 %collective-permute-done.53 = f32[32,128]{1,0:T(8,128)S(1)} collective-permute-done((f32[32,128]{1,0:T(8,128)S(1)}, f32[32,128]{1,0:T(8,128)S(1)}, u32[]{:S(2)}, u32[]{:S(2)}) %collective-permute-start.53) | collective-permute-done | bytes 16416 | tf_op jit(solution)/shard_map/ppermute | solution.py:36
  (136 shorter events, 91.6 us)
Async XLA Ops:
  6.6 6.5 %collective-permute-start.1 = (bf16[160,640]{1,0:T(8,128)(2,1)S(1)}, bf16[160,640]{1,0:T(8,128)(2,1)S(1)}, u32[]{:S(2)}, u32[]{:S(2)}) collective-permute-start(bf16[160,640]{1,0:T(8,128)(2,1)S(1)} %pad_maximum_fusion.7), channel_id=1, source_target_pairs={{0,200},{1,201},{2,202},{3,203},{4,204},{5,205},{6,206},{7,207},{8... | collective-permute-start | bytes 614408 | tf_op jit(solution)/shard_map/ppermute | solution.py:36
  13.1 7.5 %collective-permute-start.2 = (bf16[320,640]{1,0:T(8,128)(2,1)S(1)}, bf16[320,640]{1,0:T(8,128)(2,1)S(1)}, u32[]{:S(2)}, u32[]{:S(2)}) collective-permute-start(bf16[320,640]{1,0:T(8,128)(2,1)S(1)} %pad_maximum_fusion.2), channel_id=1, source_target_pairs={{0,24},{1,25},{2,26},{3,27},{4,28},{5,29},{6,30},{7,31},{8,64},{9,... | collective-permute-start | bytes 1228808 | tf_op jit(solution)/shard_map/ppermute | solution.py:36
  14.7 8.7 %collective-permute-start.6 = (bf16[320,640]{1,0:T(8,128)(2,1)S(1)}, bf16[320,640]{1,0:T(8,128)(2,1)S(1)}, u32[]{:S(2)}, u32[]{:S(2)}) collective-permute-start(bf16[320,640]{1,0:T(8,128)(2,1)S(1)} %pad_maximum_fusion.3), channel_id=1, source_target_pairs={{0,56},{1,57},{2,58},{3,59},{4,60},{5,61},{6,62},{7,63},{8,192},{9... | collective-permute-start | bytes 1228808 | tf_op jit(solution)/shard_map/ppermute | solution.py:36
  23.5 11.9 %collective-permute-start.7 = (bf16[640,640]{1,0:T(8,128)(2,1)S(1)}, bf16[640,640]{1,0:T(8,128)(2,1)S(1)}, u32[]{:S(2)}, u32[]{:S(2)}) collective-permute-start(bf16[640,640]{1,0:T(8,128)(2,1)S(1)} %get-tuple-element.48.refs_2_), channel_id=1, source_target_pairs={{0,24},{1,25},{2,26},{3,27},{4,28},{5,29},{6,30},{7,31},{8,64},{9,... | collective-permute-start | bytes 2457608 | tf_op jit(solution)/shard_map/ppermute | solution.py:36
  24.1 13.0 %collective-permute-start.3 = (bf16[640,640]{1,0:T(8,128)(2,1)S(1)}, bf16[640,640]{1,0:T(8,128)(2,1)S(1)}, u32[]{:S(2)}, u32[]{:S(2)}) collective-permute-start(bf16[640,640]{1,0:T(8,128)(2,1)S(1)} %get-tuple-element.50.refs_0_), channel_id=1, source_target_pairs={{0,56},{1,57},{2,58},{3,59},{4,60},{5,61},{6,62},{7,63},{8,192},{9... | collective-permute-start | bytes 2457608 | tf_op jit(solution)/shard_map/ppermute | solution.py:36
  26.5 11.1 %collective-permute-start.10 = (bf16[160,640]{1,0:T(8,128)(2,1)S(1)}, bf16[160,640]{1,0:T(8,128)(2,1)}, u32[]{:S(2)}, u32[]{:S(2)}) collective-permute-start(bf16[160,640]{1,0:T(8,128)(2,1)S(1)} %get-tuple-element.27), channel_id=1, source_target_pairs={{0,8},{1,9},{2,10},{3,11},{4,12},{5,13},{6,14},{7,15},{8,0},{9,1},... | collective-permute-start | bytes 614408 | tf_op jit(solution)/shard_map/ppermute | solution.py:36
  26.7 42.9 %collective-permute-start.8 = (bf16[1280,640]{1,0:T(8,128)(2,1)}, bf16[1280,640]{1,0:T(8,128)(2,1)S(1)}, u32[]{:S(2)}, u32[]{:S(2)}) collective-permute-start(bf16[1280,640]{1,0:T(8,128)(2,1)} %copy-done.1), channel_id=1, source_target_pairs={{0,8},{1,9},{2,10},{3,11},{4,12},{5,13},{6,14},{7,15},{8,0},{9,1},... | collective-permute-start | bytes 4915208 | tf_op jit(solution)/shard_map/ppermute | solution.py:36
  37.2 32.4 %collective-permute-start.9 = (bf16[1280,640]{1,0:T(8,128)(2,1)S(1)}, bf16[1280,640]{1,0:T(8,128)(2,1)S(1)}, u32[]{:S(2)}, u32[]{:S(2)}) collective-permute-start(bf16[1280,640]{1,0:T(8,128)(2,1)S(1)} %pad_maximum_fusion), channel_id=1, source_target_pairs={{0,8},{1,9},{2,10},{3,11},{4,12},{5,13},{6,14},{7,15},{8,0},{9,1},... | collective-permute-start | bytes 4915208 | tf_op jit(solution)/shard_map/ppermute | solution.py:36
  43.9 9.7 %collective-permute-start.12 = (bf16[320,640]{1,0:T(8,128)(2,1)S(1)}, bf16[320,640]{1,0:T(8,128)(2,1)S(1)}, u32[]{:S(2)}, u32[]{:S(2)}) collective-permute-start(bf16[320,640]{1,0:T(8,128)(2,1)S(1)} %pad_maximum_fusion.4.refs_6_), channel_id=1, source_target_pairs={{0,15},{1,8},{2,9},{3,10},{4,11},{5,12},{6,13},{7,14},{8,1},{9,2},... | collective-permute-start | bytes 1228808 | tf_op jit(solution)/shard_map/ppermute | solution.py:36
  53.6 7.4 %collective-permute-start.13 = (bf16[320,640]{1,0:T(8,128)(2,1)S(1)}, bf16[320,640]{1,0:T(8,128)(2,1)S(1)}, u32[]{:S(2)}, u32[]{:S(2)}) collective-permute-start(bf16[320,640]{1,0:T(8,128)(2,1)S(1)} %collective-permute-done.12.refs_7_), channel_id=1, source_target_pairs={{0,9},{1,10},{2,11},{3,12},{4,13},{5,14},{6,15},{7,8},{8,7},{9,0},... | collective-permute-start | bytes 1228808 | tf_op jit(solution)/shard_map/ppermute | solution.py:36
  60.9 8.7 %collective-permute-start.14 = (bf16[320,640]{1,0:T(8,128)(2,1)S(1)}, bf16[320,640]{1,0:T(8,128)(2,1)S(1)}, u32[]{:S(2)}, u32[]{:S(2)}) collective-permute-start(bf16[320,640]{1,0:T(8,128)(2,1)S(1)} %collective-permute-done.13.refs_8_), channel_id=1, source_target_pairs={{0,15},{1,8},{2,9},{3,10},{4,11},{5,12},{6,13},{7,14},{8,1},{9,2},... | collective-permute-start | bytes 1228808 | tf_op jit(solution)/shard_map/ppermute | solution.py:36
  75.0 7.0 %collective-permute-start.19 = (bf16[80,640]{1,0:T(8,128)(2,1)S(1)}, bf16[80,640]{1,0:T(8,128)(2,1)S(1)}, u32[]{:S(2)}, u32[]{:S(2)}) collective-permute-start(bf16[80,640]{1,0:T(8,128)(2,1)S(1)} %get-tuple-element.30), channel_id=1, source_target_pairs={{0,9},{1,10},{2,11},{3,12},{4,13},{5,14},{6,15},{7,8},{8,7},{9,0},... | collective-permute-start | bytes 307208 | tf_op jit(solution)/shard_map/ppermute | solution.py:36
  78.6 7.2 %collective-permute-start.16 = (bf16[192,640]{1,0:T(8,128)(2,1)S(1)}, bf16[192,640]{1,0:T(8,128)(2,1)S(1)}, u32[]{:S(2)}, u32[]{:S(2)}) collective-permute-start(bf16[192,640]{1,0:T(8,128)(2,1)S(1)} %constant_dynamic-update-slice_fusion.16.refs_0_), channel_id=1, source_target_pairs={{0,15},{1,8},{2,9},{3,10},{4,11},{5,12},{6,13},{7,14},{8,1},{9,2},... | collective-permute-start | bytes 737288 | tf_op jit(solution)/shard_map/ppermute | solution.py:36
  88.1 6.7 %collective-permute-start.21 = (bf16[160,640]{1,0:T(8,128)(2,1)S(1)}, bf16[160,640]{1,0:T(8,128)(2,1)S(1)}, u32[]{:S(2)}, u32[]{:S(2)}) collective-permute-start(bf16[160,640]{1,0:T(8,128)(2,1)S(1)} %collective-permute-done.20.refs_5_), channel_id=1, source_target_pairs={{0,9},{1,10},{2,11},{3,12},{4,13},{5,14},{6,15},{7,8},{8,7},{9,0},... | collective-permute-start | bytes 614408 | tf_op jit(solution)/shard_map/ppermute | solution.py:36
  91.5 9.3 %collective-permute-start.18 = (bf16[192,640]{1,0:T(8,128)(2,1)S(1)}, bf16[192,640]{1,0:T(8,128)(2,1)S(1)}, u32[]{:S(2)}, u32[]{:S(2)}) collective-permute-start(bf16[192,640]{1,0:T(8,128)(2,1)S(1)} %collective-permute-done.17.refs_2_), channel_id=1, source_target_pairs={{0,15},{1,8},{2,9},{3,10},{4,11},{5,12},{6,13},{7,14},{8,1},{9,2},... | collective-permute-start | bytes 737288 | tf_op jit(solution)/shard_map/ppermute | solution.py:36
  104.0 6.4 %collective-permute-start.27 = (bf16[80,640]{1,0:T(8,128)(2,1)S(1)}, bf16[80,640]{1,0:T(8,128)(2,1)S(1)}, u32[]{:S(2)}, u32[]{:S(2)}) collective-permute-start(bf16[80,640]{1,0:T(8,128)(2,1)S(1)} %get-tuple-element.32), channel_id=1, source_target_pairs={{0,200},{1,201},{2,202},{3,203},{4,204},{5,205},{6,206},{7,207},{8... | collective-permute-start | bytes 307208 | tf_op jit(solution)/shard_map/ppermute | solution.py:36
  108.1 6.5 %collective-permute-start.24 = (bf16[160,640]{1,0:T(8,128)(2,1)S(1)}, bf16[160,640]{1,0:T(8,128)(2,1)S(1)}, u32[]{:S(2)}, u32[]{:S(2)}) collective-permute-start(bf16[160,640]{1,0:T(8,128)(2,1)S(1)} %pad_maximum_fusion.9), channel_id=1, source_target_pairs={{0,200},{1,201},{2,202},{3,203},{4,204},{5,205},{6,206},{7,207},{8... | collective-permute-start | bytes 614408 | tf_op jit(solution)/shard_map/ppermute | solution.py:36
  114.6 7.5 %collective-permute-start.25 = (bf16[320,640]{1,0:T(8,128)(2,1)S(1)}, bf16[320,640]{1,0:T(8,128)(2,1)S(1)}, u32[]{:S(2)}, u32[]{:S(2)}) collective-permute-start(bf16[320,640]{1,0:T(8,128)(2,1)S(1)} %pad_maximum_fusion.5), channel_id=1, source_target_pairs={{0,24},{1,25},{2,26},{3,27},{4,28},{5,29},{6,30},{7,31},{8,64},{9,... | collective-permute-start | bytes 1228808 | tf_op jit(solution)/shard_map/ppermute | solution.py:36
  115.7 8.7 %collective-permute-start.29 = (bf16[320,640]{1,0:T(8,128)(2,1)S(1)}, bf16[320,640]{1,0:T(8,128)(2,1)S(1)}, u32[]{:S(2)}, u32[]{:S(2)}) collective-permute-start(bf16[320,640]{1,0:T(8,128)(2,1)S(1)} %pad_maximum_fusion.6), channel_id=1, source_target_pairs={{0,56},{1,57},{2,58},{3,59},{4,60},{5,61},{6,62},{7,63},{8,192},{9... | collective-permute-start | bytes 1228808 | tf_op jit(solution)/shard_map/ppermute | solution.py:36
  124.5 11.9 %collective-permute-start.30 = (bf16[640,640]{1,0:T(8,128)(2,1)S(1)}, bf16[640,640]{1,0:T(8,128)(2,1)S(1)}, u32[]{:S(2)}, u32[]{:S(2)}) collective-permute-start(bf16[640,640]{1,0:T(8,128)(2,1)S(1)} %get-tuple-element.44.refs_2_), channel_id=1, source_target_pairs={{0,24},{1,25},{2,26},{3,27},{4,28},{5,29},{6,30},{7,31},{8,64},{9,... | collective-permute-start | bytes 2457608 | tf_op jit(solution)/shard_map/ppermute | solution.py:36
  124.6 13.1 %collective-permute-start.26 = (bf16[640,640]{1,0:T(8,128)(2,1)S(1)}, bf16[640,640]{1,0:T(8,128)(2,1)S(1)}, u32[]{:S(2)}, u32[]{:S(2)}) collective-permute-start(bf16[640,640]{1,0:T(8,128)(2,1)S(1)} %get-tuple-element.46.refs_0_), channel_id=1, source_target_pairs={{0,56},{1,57},{2,58},{3,59},{4,60},{5,61},{6,62},{7,63},{8,192},{9... | collective-permute-start | bytes 2457608 | tf_op jit(solution)/shard_map/ppermute | solution.py:36
  126.7 42.4 %collective-permute-start.31 = (bf16[1280,640]{1,0:T(8,128)(2,1)S(1)}, bf16[1280,640]{1,0:T(8,128)(2,1)S(1)}, u32[]{:S(2)}, u32[]{:S(2)}) collective-permute-start(bf16[1280,640]{1,0:T(8,128)(2,1)S(1)} %get-tuple-element.43), channel_id=1, source_target_pairs={{0,8},{1,9},{2,10},{3,11},{4,12},{5,13},{6,14},{7,15},{8,0},{9,1},... | collective-permute-start | bytes 4915208 | tf_op jit(solution)/shard_map/ppermute | solution.py:36
  137.8 31.3 %collective-permute-start.32 = (bf16[1280,640]{1,0:T(8,128)(2,1)S(1)}, bf16[1280,640]{1,0:T(8,128)(2,1)S(1)}, u32[]{:S(2)}, u32[]{:S(2)}) collective-permute-start(bf16[1280,640]{1,0:T(8,128)(2,1)S(1)} %pad_maximum_fusion.1), channel_id=1, source_target_pairs={{0,8},{1,9},{2,10},{3,11},{4,12},{5,13},{6,14},{7,15},{8,0},{9,1},... | collective-permute-start | bytes 4915208 | tf_op jit(solution)/shard_map/ppermute | solution.py:36
  143.5 9.3 %collective-permute-start.34 = (bf16[320,640]{1,0:T(8,128)(2,1)S(1)}, bf16[320,640]{1,0:T(8,128)(2,1)S(1)}, u32[]{:S(2)}, u32[]{:S(2)}) collective-permute-start(bf16[320,640]{1,0:T(8,128)(2,1)S(1)} %constant_dynamic-update-slice_fusion.36.refs_6_), channel_id=1, source_target_pairs={{0,15},{1,8},{2,9},{3,10},{4,11},{5,12},{6,13},{7,14},{8,1},{9,2},... | collective-permute-start | bytes 1228808 | tf_op jit(solution)/shard_map/ppermute | solution.py:36
  152.8 7.4 %collective-permute-start.35 = (bf16[320,640]{1,0:T(8,128)(2,1)S(1)}, bf16[320,640]{1,0:T(8,128)(2,1)S(1)}, u32[]{:S(2)}, u32[]{:S(2)}) collective-permute-start(bf16[320,640]{1,0:T(8,128)(2,1)S(1)} %collective-permute-done.34.refs_7_), channel_id=1, source_target_pairs={{0,9},{1,10},{2,11},{3,12},{4,13},{5,14},{6,15},{7,8},{8,7},{9,0},... | collective-permute-start | bytes 1228808 | tf_op jit(solution)/shard_map/ppermute | solution.py:36
  160.2 8.9 %collective-permute-start.36 = (bf16[320,640]{1,0:T(8,128)(2,1)S(1)}, bf16[320,640]{1,0:T(8,128)(2,1)S(1)}, u32[]{:S(2)}, u32[]{:S(2)}) collective-permute-start(bf16[320,640]{1,0:T(8,128)(2,1)S(1)} %collective-permute-done.35.refs_8_), channel_id=1, source_target_pairs={{0,15},{1,8},{2,9},{3,10},{4,11},{5,12},{6,13},{7,14},{8,1},{9,2},... | collective-permute-start | bytes 1228808 | tf_op jit(solution)/shard_map/ppermute | solution.py:36
  172.8 10.0 %collective-permute-start.37 = (bf16[80,640]{1,0:T(8,128)(2,1)S(1)}, bf16[80,640]{1,0:T(8,128)(2,1)S(1)}, u32[]{:S(2)}, u32[]{:S(2)}) collective-permute-start(bf16[80,640]{1,0:T(8,128)(2,1)S(1)} %get-tuple-element.36), channel_id=1, source_target_pairs={{0,9},{1,10},{2,11},{3,12},{4,13},{5,14},{6,15},{7,8},{8,7},{9,0},... | collective-permute-start | bytes 307208 | tf_op jit(solution)/shard_map/ppermute | solution.py:36
  178.1 8.1 %collective-permute-start.42 = (bf16[160,640]{1,0:T(8,128)(2,1)S(1)}, bf16[160,640]{1,0:T(8,128)(2,1)S(1)}, u32[]{:S(2)}, u32[]{:S(2)}) collective-permute-start(bf16[160,640]{1,0:T(8,128)(2,1)S(1)} %constant_dynamic-update-slice_fusion.40.refs_4_), channel_id=1, source_target_pairs={{0,15},{1,8},{2,9},{3,10},{4,11},{5,12},{6,13},{7,14},{8,1},{9,2},... | collective-permute-start | bytes 614408 | tf_op jit(solution)/shard_map/ppermute | solution.py:36
  191.4 7.1 %collective-permute-start.44 = (bf16[160,640]{1,0:T(8,128)(2,1)S(1)}, bf16[160,640]{1,0:T(8,128)(2,1)S(1)}, u32[]{:S(2)}, u32[]{:S(2)}) collective-permute-start(bf16[160,640]{1,0:T(8,128)(2,1)S(1)} %collective-permute-done.43.refs_6_), channel_id=1, source_target_pairs={{0,15},{1,8},{2,9},{3,10},{4,11},{5,12},{6,13},{7,14},{8,1},{9,2},... | collective-permute-start | bytes 614408 | tf_op jit(solution)/shard_map/ppermute | solution.py:36
  194.6 7.3 %collective-permute-start.40 = (bf16[160,640]{1,0:T(8,128)(2,1)S(1)}, bf16[160,640]{1,0:T(8,128)(2,1)S(1)}, u32[]{:S(2)}, u32[]{:S(2)}) collective-permute-start(bf16[160,640]{1,0:T(8,128)(2,1)S(1)} %collective-permute-done.39.refs_2_), channel_id=1, source_target_pairs={{0,15},{1,8},{2,9},{3,10},{4,11},{5,12},{6,13},{7,14},{8,1},{9,2},... | collective-permute-start | bytes 614408 | tf_op jit(solution)/shard_map/ppermute | solution.py:36
  204.8 32.5 %collective-permute-start.45 = (f32[160,640]{1,0:T(8,128)S(1)}, f32[160,640]{1,0:T(8,128)S(1)}, u32[]{:S(2)}, u32[]{:S(2)}) collective-permute-start(f32[160,640]{1,0:T(8,128)S(1)} %get-tuple-element.39), channel_id=1, source_target_pairs={{0,8},{1,9},{2,10},{3,11},{4,12},{5,13},{6,14},{7,15},{8,0},{9,1},... | collective-permute-start | bytes 1228808 | tf_op jit(solution)/shard_map/ppermute | solution.py:36
  229.0 7.2 %collective-permute-start.53 = (f32[32,128]{1,0:T(8,128)S(1)}, f32[32,128]{1,0:T(8,128)S(1)}, u32[]{:S(2)}, u32[]{:S(2)}) collective-permute-start(f32[32,128]{1,0:T(8,128)S(1)} %add.61), channel_id=1, source_target_pairs={{0,12},{1,13},{2,14},{3,15},{4,8},{5,9},{6,10},{7,11},{8,4},{9,5},... | collective-permute-start | bytes 49160 | tf_op jit(solution)/shard_map/ppermute | solution.py:36
  (24 other events, 107.2 us)
where the time goes:
time: 241 us; the launch traced here: 238 us
  waiting for transfers between devices  138 us (57%)
  starting transfers between devices  79 us (33%)
  Pallas kernels  14.2 us (6%)
  local copies, waits for them, and re-layouts  3.54 us (1%)
  other arithmetic  2.55 us (1%)
    ppermute x54, waiting for transfers between devices, permute(): lax.ppermute(value, AXES, [(rank(*d), rank(*target(*d))) for d in EVERY])  138 us
    ppermute x54, starting transfers between devices, permute(): lax.ppermute(value, AXES, [(rank(*d), rank(*target(*d))) for d in EVERY])  79 us
    pallas_call x2, Pallas kernels, first_product(): pl.pallas_call(functools.partial(first_body, step, len(right), len(left))...  8.28 us
    pallas_call x2, Pallas kernels, second_product(): pl.pallas_call(functools.partial(second_body, last, len(left)), out_shape...  5.89 us
  transfers between devices with their start and end apart: 54, of which 39 were waited for; matrix products, arithmetic and copies ran while one was open for 1% of the time, Pallas kernels for 0%

commit v1 on v0

--- a/solution.py
+++ b/solution.py
@@ -248,72 +248,94 @@
     )(order, *right, *left)
 
 
-def second_body(last, n_left, order, shift, panel, current, *refs):
-    left = refs[:n_left]
-    outs = refs[n_left:]
-    if last:
-        earlier, outs = outs[0], outs[1:]
-    wide, summed = outs[-2], outs[-1]
-    rows, cols = current.shape
-    half = rows // 2
-    lay_rows(order, left[: n_left // 2], wide, 0, half)
-    lay_rows(order, left[n_left // 2 :], wide, half, half)
+def second_body(step, part, order, shift, panel, current, *refs):
+    left, refs = refs[:4], list(refs[4:])
+    half, cols = refs[-1].shape
+    wide, summed = refs[-2:]
+    taken = 0
+    if part:
+        stats_top = refs[0]
+        taken = 1
+        if step == 0:
+            scale_in = refs[1]
+        else:
+            stats_first = refs[1]
+        above = refs[2]
+        taken = 3
+    outs = refs[taken:-2]
+    lay_rows(order, left, wide, 0, half)
     multiply(wide, panel, summed)
-    value = 1.5 * current[...].astype(jnp.float32)
-    if last:
+    first = part * half if current.shape[0] > half else 0
+    value = 1.5 * current[first : first + half, :].astype(jnp.float32)
+    if step == 1:
         value = value - 0.5 * summed[...]
     else:
-        partial = jnp.zeros((8, 128), jnp.float32)
-        for piece in left[: n_left // 2]:
-            for k in range(2):
-                partial = partial + read_parts(piece, k * (half + EXTRA) + half)
-        squares = jnp.sum(jnp.sum(partial, axis=0, keepdims=True), axis=1, keepdims=True)
-        scale = TARGET * (cols * NZ) / (squares + 1e-06)
+        if part:
+            scale = scale_in[:1, :1]
+        else:
+            partial = jnp.zeros((8, 128), jnp.float32)
+            for piece in left:
+                for k in range(2):
+                    partial = partial + read_parts(piece, k * (half + EXTRA) + half)
+            squares = jnp.sum(jnp.sum(partial, axis=0, keepdims=True), axis=1, keepdims=True)
+            scale = TARGET * (cols * NZ) / (squares + 1e-06)
+            outs[3][...] = jnp.broadcast_to(scale, (8, 128))
         value = jnp.sqrt(scale) * (value - 0.5 * (scale * summed[...]))
-    outs[0][...] = value
-    r = lax.broadcasted_iota(jnp.int32, (rows, cols), 0)
-    k = lax.broadcasted_iota(jnp.int32, (rows, cols), 1)
+    if step and part:
+        outs[0][:half, :] = above[...]
+        outs[0][half:, :] = value
+    else:
+        outs[0][...] = value
+    r = lax.broadcasted_iota(jnp.int32, (half, cols), 0) + part * half
+    k = lax.broadcasted_iota(jnp.int32, (half, cols), 1)
     diagonal = fold(jnp.where(k - r == shift[0], value, 0.0))
     power = fold(value * value)
+    if part:
+        diagonal = diagonal + stats_top[:8, :]
+        power = power + stats_top[8:, :]
     stats = outs[1]
-    if last:
-        stats[:16, :] = earlier[...]
-        stats[16:24, :] = diagonal
-        stats[24:, :] = power
-    else:
-        stats[:8, :] = diagonal
-        stats[8:, :] = power
+    base = 0
+    if step and part:
+        stats[:16, :] = stats_first[...]
+        base = 16
+    stats[base : base + 8, :] = diagonal
+    stats[base + 8 : base + 16, :] = power
+    if step == 0:
         rounded = value.astype(jnp.bfloat16)
         outs[2][...] = rounded
-        outs[3][...] = rounded[: rows // 2]
-        outs[4][...] = rounded[rows // 2 :]
-
-
-def second_product(order, shift, panel, current, left, earlier):
-    last = earlier is not None
-    more = [earlier] if last else []
-    rows, cols = current.shape
+        if part:
+            outs[3][:half, :] = above[...]
+            outs[3][half:, :] = rounded
+
+
+def second_product(step, part, order, shift, panel, current, left, more):
+    half, cols = left[-1].shape[0] // 2, panel.shape[1]
+    if step == 0 and part == 0:
+        half -= EXTRA
     full = cols * NZ
     shapes = [
-        jax.ShapeDtypeStruct((rows, cols), jnp.float32),
-        jax.ShapeDtypeStruct((32 if last else 16, 128), jnp.float32),
+        jax.ShapeDtypeStruct((2 * half if step and part else half, cols), jnp.float32),
+        jax.ShapeDtypeStruct((32 if step and part else 16, 128), jnp.float32),
     ]
-    if not last:
-        shapes.append(jax.ShapeDtypeStruct((rows, cols), jnp.bfloat16))
-        shapes += [jax.ShapeDtypeStruct((rows // 2, cols), jnp.bfloat16)] * 2
+    if step == 0:
+        shapes.append(jax.ShapeDtypeStruct((half, cols), jnp.bfloat16))
+        if part == 0:
+            shapes.append(jax.ShapeDtypeStruct((8, 128), jnp.float32))
+        else:
+            shapes.append(jax.ShapeDtypeStruct((2 * half, cols), jnp.bfloat16))
     return pl.pallas_call(
-        functools.partial(second_body, last, len(left)),
+        functools.partial(second_body, step, part),
         out_shape=shapes,
         in_specs=[smem()] * 2 + [vmem()] * (2 + len(left) + len(more)),
         out_specs=[vmem()] * len(shapes),
         scratch_shapes=[
-            pltpu.VMEM((rows, full), jnp.bfloat16),
-            pltpu.VMEM((rows, cols), jnp.float32),
+            pltpu.VMEM((half, full), jnp.bfloat16),
+            pltpu.VMEM((half, cols), jnp.float32),
         ],
         name="second_product",
         compiler_params=pltpu.CompilerParams(vmem_limit_bytes=14 * 2**20),
         cost_estimate=pl.CostEstimate(
-            flops=2 * rows * cols * full, bytes_accessed=2 * full * cols, transcendentals=0
+            flops=2 * half * cols * full, bytes_accessed=2 * full * cols, transcendentals=0
         ),
     )(order, shift, panel, current, *left, *more)
 
@@ -340,9 +362,9 @@
             if turn < 3:
                 part = join(part, moved)
         right += [part, moved]
-    first = permute(join(right[0], right[2]), to_sibling)
-    second = permute(join(right[1], right[3]), to_sibling)
-    return right + [first, second], left
+    swaps = (join(right[0], right[2]), right[1], right[3])
+    right += [permute(value, to_sibling) for value in swaps]
+    return right, left
 
 
 def row_panel(top, bottom):
@@ -366,11 +388,10 @@
 
 
 def totals(stats):
-    stats = stats + permute(stats, to_sibling)
-    for k in range(4):
-        stats = stats + permute(stats, row_target(k // 2, k % 2))
-    for step in (1, 2, 4):
-        stats = stats + permute(stats, lambda x, y, c, z: (x, y, 1 - c, z ^ step))
+    targets = [to_sibling] + [row_target(k // 2, k % 2) for k in range(4)]
+    targets += [lambda x, y, c, z, step=step: (x, y, 1 - c, z ^ step) for step in (1, 2, 4)]
+    for target in targets:
+        stats = stats + permute(stats, target)
     return jnp.sum(stats.reshape(2, 2, 8, 128), axis=(2, 3))
 
 
@@ -383,19 +404,26 @@
     core = jnp.bitwise_xor(lax.axis_index("c"), z % 2)
     row_first = (lax.axis_index(("x", "y")) * NC + core) * rows
     shift = (row_first - z * cols).reshape(1)
-    order, shift, matrix = in_step(order, shift, matrix)
     tile, top, bottom = prepare(matrix)
 
     tile = jnp.where(moved_row, permute(tile, to_sibling), tile)
+    order, shift, tile = in_step(order, shift, tile)
     right, left = panels(tile, top, bottom)
     s_top, s_bottom, panel = first_product(0, order, right, left, rows, cols)
     left = row_panel(s_top, s_bottom)
-    current, stats, tile, top, bottom = second_product(order, shift, panel, tile, left, None)
+    cur_top, stats_top, top, scale = second_product(0, 0, order, shift, panel, tile, left[:4], [])
+    cur_bottom, stats_first, bottom, tile = second_product(
+        0, 1, order, shift, panel, tile, left[4:], [stats_top, scale, top]
+    )
     right, left = panels(tile, top, bottom)
     s_top, s_bottom, panel = first_product(1, order, right, left, rows, cols)
     left = row_panel(s_top, s_bottom)
-    current, stats = second_product(order, shift, panel, current, left, stats)
-    current = jnp.where(moved_row, permute(current, to_sibling), current)
+    above, stats_top = second_product(1, 0, order, shift, panel, cur_top, left[:4], [])
+    current, stats = second_product(
+        1, 1, order, shift, panel, cur_bottom, left[4:], [stats_top, stats_first, above]
+    )
+    other = permute(current, to_sibling)
+    current = jnp.where(moved_row, other, current)
     sums = totals(stats)
     return (current, sums[:, 0], jnp.sqrt(sums[:, 1]))
 

time: 241 us -> 219 us (0.909)
  waiting for transfers between devices: 138 us -> 102 us
  starting transfers between devices: 79 us -> 84.7 us
  local copies, waits for them, and re-layouts: 3.54 us -> 8.86 us
  Pallas kernels: 14.2 us -> 18.1 us
    ppermute x54 -> x56, waiting for transfers between devices: 138 us -> 102 us  [permute(): lax.ppermute(value, AXES, [(rank(*d), rank(*target(*d))) for d in EVERY])]
    ppermute x54 -> x56, starting transfers between devices: 79 us -> 84.7 us  [permute(): lax.ppermute(value, AXES, [(rank(*d), rank(*target(*d))) for d in EVERY])]
    unnamed x23 -> x22, local copies, waits for them, and re-layouts: 1.7 us -> 6.3 us
    pallas_call x2 -> x4, Pallas kernels: 5.89 us -> 9.84 us  [second_product(): pl.pallas_call(functools.partial(second_body, step, part), out_shape=shap...]
  transfers between devices with their start and end apart: 54 -> 56, of which waited for: 39 -> 36; matrix products, arithmetic and copies ran while one was open for 1% -> 4% of each run, Pallas kernels for 0% -> 3%
where the time goes in v1:
time: 219 us; the launch traced here: 216 us
  waiting for transfers between devices  102 us (47%)
  starting transfers between devices  84.7 us (39%)
  Pallas kernels  18.1 us (8%)
  local copies, waits for them, and re-layouts  8.86 us (4%)
    ppermute x56, waiting for transfers between devices, permute(): lax.ppermute(value, AXES, [(rank(*d), rank(*target(*d))) for d in EVERY])  102 us
    ppermute x56, starting transfers between devices, permute(): lax.ppermute(value, AXES, [(rank(*d), rank(*target(*d))) for d in EVERY])  84.7 us
    pallas_call x4, Pallas kernels, second_product(): pl.pallas_call(functools.partial(second_body, step, part), out_shape=shap...  9.84 us
    pallas_call x2, Pallas kernels, first_product(): pl.pallas_call(functools.partial(first_body, step, len(right), len(left))...  8.28 us
    unnamed x22, local copies, waits for them, and re-layouts  6.3 us
  transfers between devices with their start and end apart: 56, of which 36 were waited for; matrix products, arithmetic and copies ran while one was open for 4% of the time, Pallas kernels for 3%

profile of v1, /device:TPU:32, one launch (start us, length us, event | category | flops | bytes accessed | tf_op | source)
XLA Modules:
  0.0 216.1 jit_solution(13244833844287088640)
XLA Ops:
  5.9 2.6 %collective-permute-start.2 = (bf16[160,640]{1,0:T(8,128)(2,1)S(1)}, bf16[160,640]{1,0:T(8,128)(2,1)S(1)}, u32[]{:S(2)}, u32[]{:S(2)}) collective-permute-start(bf16[160,640]{1,0:T(8,128)(2,1)S(1)} %pad_maximum_fusion.4), channel_id=1, source_target_pairs={{0,200},{1,201},{2,202},{3,203},{4,204},{5,205},{6,206},{7,207},{8... | collective-permute-start | bytes 614408 | tf_op jit(solution)/shard_map/ppermute | solution.py:36
  9.4 2.9 %collective-permute-done.2 = bf16[160,640]{1,0:T(8,128)(2,1)S(1)} collective-permute-done((bf16[160,640]{1,0:T(8,128)(2,1)S(1)}, bf16[160,640]{1,0:T(8,128)(2,1)S(1)}, u32[]{:S(2)}, u32[]{:S(2)}) %collective-permute-start.2) | collective-permute-done | bytes 204832 | tf_op jit(solution)/shard_map/ppermute | solution.py:36
  29.6 3.6 %collective-permute-done.12 = bf16[160,640]{1,0:T(8,128)(2,1)S(1)} collective-permute-done((bf16[160,640]{1,0:T(8,128)(2,1)S(1)}, bf16[160,640]{1,0:T(8,128)(2,1)S(1)}, u32[]{:S(2)}, u32[]{:S(2)}) %collective-permute-start.12) | collective-permute-done | bytes 204832 | tf_op jit(solution)/shard_map/ppermute | solution.py:36
  33.3 4.3 %collective-permute-start.13 = (bf16[320,640]{1,0:T(8,128)(2,1)S(1)}, bf16[320,640]{1,0:T(8,128)(2,1)S(1)}, u32[]{:S(2)}, u32[]{:S(2)}) collective-permute-start(bf16[320,640]{1,0:T(8,128)(2,1)S(1)} %constant_dynamic-update-slice_fusion.16.refs_7_), channel_id=1, source_target_pairs={{0,15},{1,8},{2,9},{3,10},{4,11},{5,12},{6,13},{7,14},{8,1},{9,2},... | collective-permute-start | bytes 1228808 | tf_op jit(solution)/shard_map/ppermute | solution.py:36
  37.6 5.6 %collective-permute-done.13.refs_8_ = bf16[320,640]{1,0:T(8,128)(2,1)S(1)} collective-permute-done((bf16[320,640]{1,0:T(8,128)(2,1)S(1)}, bf16[320,640]{1,0:T(8,128)(2,1)S(1)}, u32[]{:S(2)}, u32[]{:S(2)}) %collective-permute-start.13) | collective-permute-done | bytes 409632 | tf_op jit(solution)/shard_map/ppermute | solution.py:36
  45.1 5.5 %collective-permute-done.14.refs_9_ = bf16[320,640]{1,0:T(8,128)(2,1)S(1)} collective-permute-done((bf16[320,640]{1,0:T(8,128)(2,1)S(1)}, bf16[320,640]{1,0:T(8,128)(2,1)S(1)}, u32[]{:S(2)}, u32[]{:S(2)}) %collective-permute-start.14) | collective-permute-done | bytes 409632 | tf_op jit(solution)/shard_map/ppermute | solution.py:36
  50.6 3.0 %collective-permute-start.15 = (bf16[320,640]{1,0:T(8,128)(2,1)S(1)}, bf16[320,640]{1,0:T(8,128)(2,1)S(1)}, u32[]{:S(2)}, u32[]{:S(2)}) collective-permute-start(bf16[320,640]{1,0:T(8,128)(2,1)S(1)} %collective-permute-done.14.refs_9_), channel_id=1, source_target_pairs={{0,15},{1,8},{2,9},{3,10},{4,11},{5,12},{6,13},{7,14},{8,1},{9,2},... | collective-permute-start | bytes 1228808 | tf_op jit(solution)/shard_map/ppermute | solution.py:36
  53.5 5.6 %collective-permute-done.15.refs_10_ = bf16[320,640]{1,0:T(8,128)(2,1)S(1)} collective-permute-done((bf16[320,640]{1,0:T(8,128)(2,1)S(1)}, bf16[320,640]{1,0:T(8,128)(2,1)S(1)}, u32[]{:S(2)}, u32[]{:S(2)}) %collective-permute-start.15) | collective-permute-done | bytes 409632 | tf_op jit(solution)/shard_map/ppermute | solution.py:36
  59.2 4.6 %first_product.2 = (bf16[96,640]{1,0:T(8,128)(2,1)S(1)}, bf16[80,640]{1,0:T(8,128)(2,1)S(1)}, bf16[5120,640]{1,0:T(8,128)(2,1)S(1)}) custom-call(s32[136]{0:T(256)S(1)} %bitcast.2, bf16[640,640]{1,0:T(8,128)(2,1)S(1)} %get-tuple-element.60.refs_0_, bf16[640,640]{1,0:T(8,128)(2,1)S(1)} %collective-permute-done.4.refs_1_, ...), custom_call_target="tpu_custom_call" | custom-call | flops 1048576000 | bytes 6553600 | tf_op jit(solution)/shard_map/first_product/pallas_call | solution.py:234
  68.2 3.0 %collective-permute-start.17 = (bf16[192,640]{1,0:T(8,128)(2,1)S(1)}, bf16[192,640]{1,0:T(8,128)(2,1)S(1)}, u32[]{:S(2)}, u32[]{:S(2)}) collective-permute-start(bf16[192,640]{1,0:T(8,128)(2,1)S(1)} %constant_dynamic-update-slice_fusion.18.refs_0_), channel_id=1, source_target_pairs={{0,15},{1,8},{2,9},{3,10},{4,11},{5,12},{6,13},{7,14},{8,1},{9,2},... | collective-permute-start | bytes 737288 | tf_op jit(solution)/shard_map/ppermute | solution.py:36
  71.3 2.6 %collective-permute-start.25 = (bf16[160,640]{1,0:T(8,128)(2,1)S(1)}, bf16[160,640]{1,0:T(8,128)(2,1)S(1)}, u32[]{:S(2)}, u32[]{:S(2)}) collective-permute-start(bf16[160,640]{1,0:T(8,128)(2,1)S(1)} %constant_dynamic-update-slice_fusion.24.refs_0_), channel_id=1, source_target_pairs={{0,15},{1,8},{2,9},{3,10},{4,11},{5,12},{6,13},{7,14},{8,1},{9,2},... | collective-permute-start | bytes 614408 | tf_op jit(solution)/shard_map/ppermute | solution.py:36
  80.8 3.1 %collective-permute-start.19 = (bf16[192,640]{1,0:T(8,128)(2,1)S(1)}, bf16[192,640]{1,0:T(8,128)(2,1)S(1)}, u32[]{:S(2)}, u32[]{:S(2)}) collective-permute-start(bf16[192,640]{1,0:T(8,128)(2,1)S(1)} %collective-permute-done.18.refs_2_), channel_id=1, source_target_pairs={{0,15},{1,8},{2,9},{3,10},{4,11},{5,12},{6,13},{7,14},{8,1},{9,2},... | collective-permute-start | bytes 737288 | tf_op jit(solution)/shard_map/ppermute | solution.py:36
  103.7 4.6 %collective-permute-start.30 = (bf16[320,640]{1,0:T(8,128)(2,1)S(1)}, bf16[320,640]{1,0:T(8,128)(2,1)S(1)}, u32[]{:S(2)}, u32[]{:S(2)}) collective-permute-start(bf16[320,640]{1,0:T(8,128)(2,1)S(1)} %pad_maximum_fusion.3), channel_id=1, source_target_pairs={{0,56},{1,57},{2,58},{3,59},{4,60},{5,61},{6,62},{7,63},{8,192},{9... | collective-permute-start | bytes 1228808 | tf_op jit(solution)/shard_map/ppermute | solution.py:36
  109.7 4.2 %collective-permute-done.30 = bf16[320,640]{1,0:T(8,128)(2,1)S(1)} collective-permute-done((bf16[320,640]{1,0:T(8,128)(2,1)S(1)}, bf16[320,640]{1,0:T(8,128)(2,1)S(1)}, u32[]{:S(2)}, u32[]{:S(2)}) %collective-permute-start.30) | collective-permute-done | bytes 409632 | tf_op jit(solution)/shard_map/ppermute | solution.py:36
  114.1 3.0 %collective-permute-start.23 = (bf16[640,640]{1,0:T(8,128)(2,1)S(1)}, bf16[640,640]{1,0:T(8,128)(2,1)S(1)}, u32[]{:S(2)}, u32[]{:S(2)}) collective-permute-start(bf16[640,640]{1,0:T(8,128)(2,1)S(1)} %get-tuple-element.56.refs_0_), channel_id=1, source_target_pairs={{0,56},{1,57},{2,58},{3,59},{4,60},{5,61},{6,62},{7,63},{8,192},{9... | collective-permute-start | bytes 2457608 | tf_op jit(solution)/shard_map/ppermute | solution.py:36
  117.9 4.4 %collective-permute-done.35 = bf16[160,640]{1,0:T(8,128)(2,1)S(1)} collective-permute-done((bf16[160,640]{1,0:T(8,128)(2,1)S(1)}, bf16[160,640]{1,0:T(8,128)(2,1)S(1)}, u32[]{:S(2)}, u32[]{:S(2)}) %collective-permute-start.35) | collective-permute-done | bytes 204832 | tf_op jit(solution)/shard_map/ppermute | solution.py:36
  122.4 4.0 %collective-permute-start.36 = (bf16[320,640]{1,0:T(8,128)(2,1)S(1)}, bf16[320,640]{1,0:T(8,128)(2,1)S(1)}, u32[]{:S(2)}, u32[]{:S(2)}) collective-permute-start(bf16[320,640]{1,0:T(8,128)(2,1)S(1)} %constant_dynamic-update-slice_fusion.38.refs_7_), channel_id=1, source_target_pairs={{0,15},{1,8},{2,9},{3,10},{4,11},{5,12},{6,13},{7,14},{8,1},{9,2},... | collective-permute-start | bytes 1228808 | tf_op jit(solution)/shard_map/ppermute | solution.py:36
  126.4 5.6 %collective-permute-done.36.refs_8_ = bf16[320,640]{1,0:T(8,128)(2,1)S(1)} collective-permute-done((bf16[320,640]{1,0:T(8,128)(2,1)S(1)}, bf16[320,640]{1,0:T(8,128)(2,1)S(1)}, u32[]{:S(2)}, u32[]{:S(2)}) %collective-permute-start.36) | collective-permute-done | bytes 409632 | tf_op jit(solution)/shard_map/ppermute | solution.py:36
  133.6 5.8 %collective-permute-done.37.refs_9_ = bf16[320,640]{1,0:T(8,128)(2,1)S(1)} collective-permute-done((bf16[320,640]{1,0:T(8,128)(2,1)S(1)}, bf16[320,640]{1,0:T(8,128)(2,1)S(1)}, u32[]{:S(2)}, u32[]{:S(2)}) %collective-permute-start.37) | collective-permute-done | bytes 409632 | tf_op jit(solution)/shard_map/ppermute | solution.py:36
  139.4 3.0 %collective-permute-start.38 = (bf16[320,640]{1,0:T(8,128)(2,1)S(1)}, bf16[320,640]{1,0:T(8,128)(2,1)S(1)}, u32[]{:S(2)}, u32[]{:S(2)}) collective-permute-start(bf16[320,640]{1,0:T(8,128)(2,1)S(1)} %collective-permute-done.37.refs_9_), channel_id=1, source_target_pairs={{0,15},{1,8},{2,9},{3,10},{4,11},{5,12},{6,13},{7,14},{8,1},{9,2},... | collective-permute-start | bytes 1228808 | tf_op jit(solution)/shard_map/ppermute | solution.py:36
  142.3 5.6 %collective-permute-done.38.refs_10_ = bf16[320,640]{1,0:T(8,128)(2,1)S(1)} collective-permute-done((bf16[320,640]{1,0:T(8,128)(2,1)S(1)}, bf16[320,640]{1,0:T(8,128)(2,1)S(1)}, u32[]{:S(2)}, u32[]{:S(2)}) %collective-permute-start.38) | collective-permute-done | bytes 409632 | tf_op jit(solution)/shard_map/ppermute | solution.py:36
  148.0 3.7 %first_product.3 = (bf16[80,640]{1,0:T(8,128)(2,1)S(1)}, bf16[80,640]{1,0:T(8,128)(2,1)S(1)}, bf16[5120,640]{1,0:T(8,128)(2,1)S(1)}) custom-call(s32[136]{0:T(256)S(1)} %bitcast.5, bf16[640,640]{1,0:T(8,128)(2,1)S(1)} %get-tuple-element.56.refs_0_, bf16[640,640]{1,0:T(8,128)(2,1)S(1)} %collective-permute-done.23.refs_1_, ...), custom_call_target="tpu_custom_call" | custom-call | flops 1048576000 | bytes 6553600 | tf_op jit(solution)/shard_map/first_product/pallas_call | solution.py:234
  153.6 3.3 %collective-permute-done.43 = bf16[80,640]{1,0:T(8,128)(2,1)S(1)} collective-permute-done((bf16[80,640]{1,0:T(8,128)(2,1)S(1)}, bf16[80,640]{1,0:T(8,128)(2,1)S(1)}, u32[]{:S(2)}, u32[]{:S(2)}) %collective-permute-start.43) | collective-permute-done | bytes 102432 | tf_op jit(solution)/shard_map/ppermute | solution.py:36
  157.0 3.9 %collective-permute-start.44 = (bf16[160,640]{1,0:T(8,128)(2,1)S(1)}, bf16[160,640]{1,0:T(8,128)(2,1)S(1)}, u32[]{:S(2)}, u32[]{:S(2)}) collective-permute-start(bf16[160,640]{1,0:T(8,128)(2,1)S(1)} %constant_dynamic-update-slice_fusion.42.refs_0_), channel_id=1, source_target_pairs={{0,15},{1,8},{2,9},{3,10},{4,11},{5,12},{6,13},{7,14},{8,1},{9,2},... | collective-permute-start | bytes 614408 | tf_op jit(solution)/shard_map/ppermute | solution.py:36
  161.0 3.3 %collective-permute-done.44.refs_1_ = bf16[160,640]{1,0:T(8,128)(2,1)S(1)} collective-permute-done((bf16[160,640]{1,0:T(8,128)(2,1)S(1)}, bf16[160,640]{1,0:T(8,128)(2,1)S(1)}, u32[]{:S(2)}, u32[]{:S(2)}) %collective-permute-start.44) | collective-permute-done | bytes 204832 | tf_op jit(solution)/shard_map/ppermute | solution.py:36
  169.5 3.2 %collective-permute-start.46 = (bf16[160,640]{1,0:T(8,128)(2,1)S(1)}, bf16[160,640]{1,0:T(8,128)(2,1)S(1)}, u32[]{:S(2)}, u32[]{:S(2)}) collective-permute-start(bf16[160,640]{1,0:T(8,128)(2,1)S(1)} %collective-permute-done.45.refs_2_), channel_id=1, source_target_pairs={{0,15},{1,8},{2,9},{3,10},{4,11},{5,12},{6,13},{7,14},{8,1},{9,2},... | collective-permute-start | bytes 614408 | tf_op jit(solution)/shard_map/ppermute | solution.py:36
  173.5 3.0 %collective-permute-start.42 = (bf16[160,640]{1,0:T(8,128)(2,1)S(1)}, bf16[160,640]{1,0:T(8,128)(2,1)S(1)}, u32[]{:S(2)}, u32[]{:S(2)}) collective-permute-start(bf16[160,640]{1,0:T(8,128)(2,1)S(1)} %collective-permute-done.41.refs_2_), channel_id=1, source_target_pairs={{0,15},{1,8},{2,9},{3,10},{4,11},{5,12},{6,13},{7,14},{8,1},{9,2},... | collective-permute-start | bytes 614408 | tf_op jit(solution)/shard_map/ppermute | solution.py:36
  184.3 3.1 %collective-permute-done.49 = f32[32,128]{1,0:T(8,128)S(1)} collective-permute-done((f32[32,128]{1,0:T(8,128)S(1)}, f32[32,128]{1,0:T(8,128)S(1)}, u32[]{:S(2)}, u32[]{:S(2)}) %collective-permute-start.49) | collective-permute-done | bytes 16416 | tf_op jit(solution)/shard_map/ppermute | solution.py:36
  188.6 3.1 %collective-permute-done.50 = f32[32,128]{1,0:T(8,128)S(1)} collective-permute-done((f32[32,128]{1,0:T(8,128)S(1)}, f32[32,128]{1,0:T(8,128)S(1)}, u32[]{:S(2)}, u32[]{:S(2)}) %collective-permute-start.50) | collective-permute-done | bytes 16416 | tf_op jit(solution)/shard_map/ppermute | solution.py:36
  195.8 3.9 %collective-permute-done.52 = f32[32,128]{1,0:T(8,128)S(1)} collective-permute-done((f32[32,128]{1,0:T(8,128)S(1)}, f32[32,128]{1,0:T(8,128)S(1)}, u32[]{:S(2)}, u32[]{:S(2)}) %collective-permute-start.52) | collective-permute-done | bytes 16416 | tf_op jit(solution)/shard_map/ppermute | solution.py:36
  203.1 3.8 %collective-permute-done.54 = f32[32,128]{1,0:T(8,128)S(1)} collective-permute-done((f32[32,128]{1,0:T(8,128)S(1)}, f32[32,128]{1,0:T(8,128)S(1)}, u32[]{:S(2)}, u32[]{:S(2)}) %collective-permute-start.54) | collective-permute-done | bytes 16416 | tf_op jit(solution)/shard_map/ppermute | solution.py:36
  208.5 5.8 %collective-permute-done.55 = f32[32,128]{1,0:T(8,128)S(1)} collective-permute-done((f32[32,128]{1,0:T(8,128)S(1)}, f32[32,128]{1,0:T(8,128)S(1)}, u32[]{:S(2)}, u32[]{:S(2)}) %collective-permute-start.55) | collective-permute-done | bytes 16416 | tf_op jit(solution)/shard_map/ppermute | solution.py:36
  (139 shorter events, 88.2 us)
Async XLA Ops:
  5.1 22.9 %collective-permute-start = (bf16[160,640]{1,0:T(8,128)(2,1)S(1)}, bf16[160,640]{1,0:T(8,128)(2,1)S(1)}, u32[]{:S(2)}, u32[]{:S(2)}) collective-permute-start(bf16[160,640]{1,0:T(8,128)(2,1)S(1)} %get-tuple-element.27), channel_id=1, source_target_pairs={{0,8},{1,9},{2,10},{3,11},{4,12},{5,13},{6,14},{7,15},{8,0},{9,1},... | collective-permute-start | bytes 614408 | tf_op jit(solution)/shard_map/ppermute | solution.py:36
  12.4 7.5 %collective-permute-start.3 = (bf16[320,640]{1,0:T(8,128)(2,1)S(1)}, bf16[320,640]{1,0:T(8,128)(2,1)S(1)}, u32[]{:S(2)}, u32[]{:S(2)}) collective-permute-start(bf16[320,640]{1,0:T(8,128)(2,1)S(1)} %pad_maximum_fusion), channel_id=1, source_target_pairs={{0,24},{1,25},{2,26},{3,27},{4,28},{5,29},{6,30},{7,31},{8,64},{9,... | collective-permute-start | bytes 1228808 | tf_op jit(solution)/shard_map/ppermute | solution.py:36
  15.2 8.7 %collective-permute-start.7 = (bf16[320,640]{1,0:T(8,128)(2,1)S(1)}, bf16[320,640]{1,0:T(8,128)(2,1)S(1)}, u32[]{:S(2)}, u32[]{:S(2)}) collective-permute-start(bf16[320,640]{1,0:T(8,128)(2,1)S(1)} %pad_maximum_fusion.1), channel_id=1, source_target_pairs={{0,56},{1,57},{2,58},{3,59},{4,60},{5,61},{6,62},{7,63},{8,192},{9... | collective-permute-start | bytes 1228808 | tf_op jit(solution)/shard_map/ppermute | solution.py:36
  24.7 19.0 %collective-permute-start.8 = (bf16[640,640]{1,0:T(8,128)(2,1)S(1)}, bf16[640,640]{1,0:T(8,128)(2,1)S(1)}, u32[]{:S(2)}, u32[]{:S(2)}) collective-permute-start(bf16[640,640]{1,0:T(8,128)(2,1)S(1)} %get-tuple-element.58.refs_2_), channel_id=1, source_target_pairs={{0,24},{1,25},{2,26},{3,27},{4,28},{5,29},{6,30},{7,31},{8,64},{9,... | collective-permute-start | bytes 2457608 | tf_op jit(solution)/shard_map/ppermute | solution.py:36
  25.3 19.7 %collective-permute-start.4 = (bf16[640,640]{1,0:T(8,128)(2,1)S(1)}, bf16[640,640]{1,0:T(8,128)(2,1)S(1)}, u32[]{:S(2)}, u32[]{:S(2)}) collective-permute-start(bf16[640,640]{1,0:T(8,128)(2,1)S(1)} %get-tuple-element.60.refs_0_), channel_id=1, source_target_pairs={{0,56},{1,57},{2,58},{3,59},{4,60},{5,61},{6,62},{7,63},{8,192},{9... | collective-permute-start | bytes 2457608 | tf_op jit(solution)/shard_map/ppermute | solution.py:36
  27.2 32.0 %collective-permute-start.9 = (bf16[1280,640]{1,0:T(8,128)(2,1)}, bf16[1280,640]{1,0:T(8,128)(2,1)S(1)}, u32[]{:S(2)}, u32[]{:S(2)}) collective-permute-start(bf16[1280,640]{1,0:T(8,128)(2,1)} %get-tuple-element.57), channel_id=1, source_target_pairs={{0,8},{1,9},{2,10},{3,11},{4,12},{5,13},{6,14},{7,15},{8,0},{9,1},... | collective-permute-start | bytes 4915208 | tf_op jit(solution)/shard_map/ppermute | solution.py:36
  33.3 10.0 %collective-permute-start.13 = (bf16[320,640]{1,0:T(8,128)(2,1)S(1)}, bf16[320,640]{1,0:T(8,128)(2,1)S(1)}, u32[]{:S(2)}, u32[]{:S(2)}) collective-permute-start(bf16[320,640]{1,0:T(8,128)(2,1)S(1)} %constant_dynamic-update-slice_fusion.16.refs_7_), channel_id=1, source_target_pairs={{0,15},{1,8},{2,9},{3,10},{4,11},{5,12},{6,13},{7,14},{8,1},{9,2},... | collective-permute-start | bytes 1228808 | tf_op jit(solution)/shard_map/ppermute | solution.py:36
  43.2 7.4 %collective-permute-start.14 = (bf16[320,640]{1,0:T(8,128)(2,1)S(1)}, bf16[320,640]{1,0:T(8,128)(2,1)S(1)}, u32[]{:S(2)}, u32[]{:S(2)}) collective-permute-start(bf16[320,640]{1,0:T(8,128)(2,1)S(1)} %collective-permute-done.13.refs_8_), channel_id=1, source_target_pairs={{0,9},{1,10},{2,11},{3,12},{4,13},{5,14},{6,15},{7,8},{8,7},{9,0},... | collective-permute-start | bytes 1228808 | tf_op jit(solution)/shard_map/ppermute | solution.py:36
  43.7 15.4 %collective-permute-start.11 = (bf16[640,640]{1,0:T(8,128)(2,1)S(1)}, bf16[640,640]{1,0:T(8,128)(2,1)S(1)}, u32[]{:S(2)}, u32[]{:S(2)}) collective-permute-start(bf16[640,640]{1,0:T(8,128)(2,1)S(1)} %collective-permute-done.8.refs_3_), channel_id=1, source_target_pairs={{0,8},{1,9},{2,10},{3,11},{4,12},{5,13},{6,14},{7,15},{8,0},{9,1},... | collective-permute-start | bytes 2457608 | tf_op jit(solution)/shard_map/ppermute | solution.py:36
  45.0 14.2 %collective-permute-start.10 = (bf16[640,640]{1,0:T(8,128)(2,1)S(1)}, bf16[640,640]{1,0:T(8,128)(2,1)S(1)}, u32[]{:S(2)}, u32[]{:S(2)}) collective-permute-start(bf16[640,640]{1,0:T(8,128)(2,1)S(1)} %collective-permute-done.4.refs_1_), channel_id=1, source_target_pairs={{0,8},{1,9},{2,10},{3,11},{4,12},{5,13},{6,14},{7,15},{8,0},{9,1},... | collective-permute-start | bytes 2457608 | tf_op jit(solution)/shard_map/ppermute | solution.py:36
  50.6 8.6 %collective-permute-start.15 = (bf16[320,640]{1,0:T(8,128)(2,1)S(1)}, bf16[320,640]{1,0:T(8,128)(2,1)S(1)}, u32[]{:S(2)}, u32[]{:S(2)}) collective-permute-start(bf16[320,640]{1,0:T(8,128)(2,1)S(1)} %collective-permute-done.14.refs_9_), channel_id=1, source_target_pairs={{0,15},{1,8},{2,9},{3,10},{4,11},{5,12},{6,13},{7,14},{8,1},{9,2},... | collective-permute-start | bytes 1228808 | tf_op jit(solution)/shard_map/ppermute | solution.py:36
  64.5 6.8 %collective-permute-start.24 = (bf16[80,640]{1,0:T(8,128)(2,1)S(1)}, bf16[80,640]{1,0:T(8,128)(2,1)S(1)}, u32[]{:S(2)}, u32[]{:S(2)}) collective-permute-start(bf16[80,640]{1,0:T(8,128)(2,1)S(1)} %get-tuple-element.36), channel_id=1, source_target_pairs={{0,9},{1,10},{2,11},{3,12},{4,13},{5,14},{6,15},{7,8},{8,7},{9,0},... | collective-permute-start | bytes 307208 | tf_op jit(solution)/shard_map/ppermute | solution.py:36
  68.2 6.9 %collective-permute-start.17 = (bf16[192,640]{1,0:T(8,128)(2,1)S(1)}, bf16[192,640]{1,0:T(8,128)(2,1)S(1)}, u32[]{:S(2)}, u32[]{:S(2)}) collective-permute-start(bf16[192,640]{1,0:T(8,128)(2,1)S(1)} %constant_dynamic-update-slice_fusion.18.refs_0_), channel_id=1, source_target_pairs={{0,15},{1,8},{2,9},{3,10},{4,11},{5,12},{6,13},{7,14},{8,1},{9,2},... | collective-permute-start | bytes 737288 | tf_op jit(solution)/shard_map/ppermute | solution.py:36
  77.3 6.6 %collective-permute-start.26 = (bf16[160,640]{1,0:T(8,128)(2,1)S(1)}, bf16[160,640]{1,0:T(8,128)(2,1)S(1)}, u32[]{:S(2)}, u32[]{:S(2)}) collective-permute-start(bf16[160,640]{1,0:T(8,128)(2,1)S(1)} %collective-permute-done.25.refs_1_), channel_id=1, source_target_pairs={{0,9},{1,10},{2,11},{3,12},{4,13},{5,14},{6,15},{7,8},{8,7},{9,0},... | collective-permute-start | bytes 614408 | tf_op jit(solution)/shard_map/ppermute | solution.py:36
  80.8 7.0 %collective-permute-start.19 = (bf16[192,640]{1,0:T(8,128)(2,1)S(1)}, bf16[192,640]{1,0:T(8,128)(2,1)S(1)}, u32[]{:S(2)}, u32[]{:S(2)}) collective-permute-start(bf16[192,640]{1,0:T(8,128)(2,1)S(1)} %collective-permute-done.18.refs_2_), channel_id=1, source_target_pairs={{0,15},{1,8},{2,9},{3,10},{4,11},{5,12},{6,13},{7,14},{8,1},{9,2},... | collective-permute-start | bytes 737288 | tf_op jit(solution)/shard_map/ppermute | solution.py:36
  83.9 6.6 %collective-permute-start.27 = (bf16[160,640]{1,0:T(8,128)(2,1)S(1)}, bf16[160,640]{1,0:T(8,128)(2,1)S(1)}, u32[]{:S(2)}, u32[]{:S(2)}) collective-permute-start(bf16[160,640]{1,0:T(8,128)(2,1)S(1)} %collective-permute-done.26.refs_2_), channel_id=1, source_target_pairs={{0,15},{1,8},{2,9},{3,10},{4,11},{5,12},{6,13},{7,14},{8,1},{9,2},... | collective-permute-start | bytes 614408 | tf_op jit(solution)/shard_map/ppermute | solution.py:36
  101.3 8.1 %collective-permute-start.22 = (bf16[320,640]{1,0:T(8,128)(2,1)S(1)}, bf16[320,640]{1,0:T(8,128)(2,1)S(1)}, u32[]{:S(2)}, u32[]{:S(2)}) collective-permute-start(bf16[320,640]{1,0:T(8,128)(2,1)S(1)} %pad_maximum_fusion.2), channel_id=1, source_target_pairs={{0,24},{1,25},{2,26},{3,27},{4,28},{5,29},{6,30},{7,31},{8,64},{9,... | collective-permute-start | bytes 1228808 | tf_op jit(solution)/shard_map/ppermute | solution.py:36
  103.7 10.2 %collective-permute-start.30 = (bf16[320,640]{1,0:T(8,128)(2,1)S(1)}, bf16[320,640]{1,0:T(8,128)(2,1)S(1)}, u32[]{:S(2)}, u32[]{:S(2)}) collective-permute-start(bf16[320,640]{1,0:T(8,128)(2,1)S(1)} %pad_maximum_fusion.3), channel_id=1, source_target_pairs={{0,56},{1,57},{2,58},{3,59},{4,60},{5,61},{6,62},{7,63},{8,192},{9... | collective-permute-start | bytes 1228808 | tf_op jit(solution)/shard_map/ppermute | solution.py:36
  114.0 18.0 %collective-permute-start.31 = (bf16[640,640]{1,0:T(8,128)(2,1)S(1)}, bf16[640,640]{1,0:T(8,128)(2,1)S(1)}, u32[]{:S(2)}, u32[]{:S(2)}) collective-permute-start(bf16[640,640]{1,0:T(8,128)(2,1)S(1)} %get-tuple-element.54.refs_2_), channel_id=1, source_target_pairs={{0,24},{1,25},{2,26},{3,27},{4,28},{5,29},{6,30},{7,31},{8,64},{9,... | collective-permute-start | bytes 2457608 | tf_op jit(solution)/shard_map/ppermute | solution.py:36
  114.1 19.4 %collective-permute-start.23 = (bf16[640,640]{1,0:T(8,128)(2,1)S(1)}, bf16[640,640]{1,0:T(8,128)(2,1)S(1)}, u32[]{:S(2)}, u32[]{:S(2)}) collective-permute-start(bf16[640,640]{1,0:T(8,128)(2,1)S(1)} %get-tuple-element.56.refs_0_), channel_id=1, source_target_pairs={{0,56},{1,57},{2,58},{3,59},{4,60},{5,61},{6,62},{7,63},{8,192},{9... | collective-permute-start | bytes 2457608 | tf_op jit(solution)/shard_map/ppermute | solution.py:36
  117.1 30.8 %collective-permute-start.32 = (bf16[1280,640]{1,0:T(8,128)(2,1)S(1)}, bf16[1280,640]{1,0:T(8,128)(2,1)S(1)}, u32[]{:S(2)}, u32[]{:S(2)}) collective-permute-start(bf16[1280,640]{1,0:T(8,128)(2,1)S(1)} %get-tuple-element.53), channel_id=1, source_target_pairs={{0,8},{1,9},{2,10},{3,11},{4,12},{5,13},{6,14},{7,15},{8,0},{9,1},... | collective-permute-start | bytes 4915208 | tf_op jit(solution)/shard_map/ppermute | solution.py:36
  122.4 9.6 %collective-permute-start.36 = (bf16[320,640]{1,0:T(8,128)(2,1)S(1)}, bf16[320,640]{1,0:T(8,128)(2,1)S(1)}, u32[]{:S(2)}, u32[]{:S(2)}) collective-permute-start(bf16[320,640]{1,0:T(8,128)(2,1)S(1)} %constant_dynamic-update-slice_fusion.38.refs_7_), channel_id=1, source_target_pairs={{0,15},{1,8},{2,9},{3,10},{4,11},{5,12},{6,13},{7,14},{8,1},{9,2},... | collective-permute-start | bytes 1228808 | tf_op jit(solution)/shard_map/ppermute | solution.py:36
  132.0 7.4 %collective-permute-start.37 = (bf16[320,640]{1,0:T(8,128)(2,1)S(1)}, bf16[320,640]{1,0:T(8,128)(2,1)S(1)}, u32[]{:S(2)}, u32[]{:S(2)}) collective-permute-start(bf16[320,640]{1,0:T(8,128)(2,1)S(1)} %collective-permute-done.36.refs_8_), channel_id=1, source_target_pairs={{0,9},{1,10},{2,11},{3,12},{4,13},{5,14},{6,15},{7,8},{8,7},{9,0},... | collective-permute-start | bytes 1228808 | tf_op jit(solution)/shard_map/ppermute | solution.py:36
  132.0 16.0 %collective-permute-start.34 = (bf16[640,640]{1,0:T(8,128)(2,1)S(1)}, bf16[640,640]{1,0:T(8,128)(2,1)S(1)}, u32[]{:S(2)}, u32[]{:S(2)}) collective-permute-start(bf16[640,640]{1,0:T(8,128)(2,1)S(1)} %collective-permute-done.31.refs_3_), channel_id=1, source_target_pairs={{0,8},{1,9},{2,10},{3,11},{4,12},{5,13},{6,14},{7,15},{8,0},{9,1},... | collective-permute-start | bytes 2457608 | tf_op jit(solution)/shard_map/ppermute | solution.py:36
  133.5 14.5 %collective-permute-start.33 = (bf16[640,640]{1,0:T(8,128)(2,1)S(1)}, bf16[640,640]{1,0:T(8,128)(2,1)S(1)}, u32[]{:S(2)}, u32[]{:S(2)}) collective-permute-start(bf16[640,640]{1,0:T(8,128)(2,1)S(1)} %collective-permute-done.23.refs_1_), channel_id=1, source_target_pairs={{0,8},{1,9},{2,10},{3,11},{4,12},{5,13},{6,14},{7,15},{8,0},{9,1},... | collective-permute-start | bytes 2457608 | tf_op jit(solution)/shard_map/ppermute | solution.py:36
  139.4 8.6 %collective-permute-start.38 = (bf16[320,640]{1,0:T(8,128)(2,1)S(1)}, bf16[320,640]{1,0:T(8,128)(2,1)S(1)}, u32[]{:S(2)}, u32[]{:S(2)}) collective-permute-start(bf16[320,640]{1,0:T(8,128)(2,1)S(1)} %collective-permute-done.37.refs_9_), channel_id=1, source_target_pairs={{0,15},{1,8},{2,9},{3,10},{4,11},{5,12},{6,13},{7,14},{8,1},{9,2},... | collective-permute-start | bytes 1228808 | tf_op jit(solution)/shard_map/ppermute | solution.py:36
  151.7 9.2 %collective-permute-start.39 = (bf16[80,640]{1,0:T(8,128)(2,1)S(1)}, bf16[80,640]{1,0:T(8,128)(2,1)S(1)}, u32[]{:S(2)}, u32[]{:S(2)}) collective-permute-start(bf16[80,640]{1,0:T(8,128)(2,1)S(1)} %get-tuple-element.43), channel_id=1, source_target_pairs={{0,9},{1,10},{2,11},{3,12},{4,13},{5,14},{6,15},{7,8},{8,7},{9,0},... | collective-permute-start | bytes 307208 | tf_op jit(solution)/shard_map/ppermute | solution.py:36
  157.0 7.4 %collective-permute-start.44 = (bf16[160,640]{1,0:T(8,128)(2,1)S(1)}, bf16[160,640]{1,0:T(8,128)(2,1)S(1)}, u32[]{:S(2)}, u32[]{:S(2)}) collective-permute-start(bf16[160,640]{1,0:T(8,128)(2,1)S(1)} %constant_dynamic-update-slice_fusion.42.refs_0_), channel_id=1, source_target_pairs={{0,15},{1,8},{2,9},{3,10},{4,11},{5,12},{6,13},{7,14},{8,1},{9,2},... | collective-permute-start | bytes 614408 | tf_op jit(solution)/shard_map/ppermute | solution.py:36
  166.8 6.7 %collective-permute-start.41 = (bf16[160,640]{1,0:T(8,128)(2,1)S(1)}, bf16[160,640]{1,0:T(8,128)(2,1)S(1)}, u32[]{:S(2)}, u32[]{:S(2)}) collective-permute-start(bf16[160,640]{1,0:T(8,128)(2,1)S(1)} %collective-permute-done.40.refs_1_), channel_id=1, source_target_pairs={{0,9},{1,10},{2,11},{3,12},{4,13},{5,14},{6,15},{7,8},{8,7},{9,0},... | collective-permute-start | bytes 614408 | tf_op jit(solution)/shard_map/ppermute | solution.py:36
  169.5 7.0 %collective-permute-start.46 = (bf16[160,640]{1,0:T(8,128)(2,1)S(1)}, bf16[160,640]{1,0:T(8,128)(2,1)S(1)}, u32[]{:S(2)}, u32[]{:S(2)}) collective-permute-start(bf16[160,640]{1,0:T(8,128)(2,1)S(1)} %collective-permute-done.45.refs_2_), channel_id=1, source_target_pairs={{0,15},{1,8},{2,9},{3,10},{4,11},{5,12},{6,13},{7,14},{8,1},{9,2},... | collective-permute-start | bytes 614408 | tf_op jit(solution)/shard_map/ppermute | solution.py:36
  182.3 33.0 %collective-permute-start.47 = (f32[160,640]{1,0:T(8,128)S(1)}, f32[160,640]{1,0:T(8,128)S(1)}, u32[]{:S(2)}, u32[]{:S(2)}) collective-permute-start(f32[160,640]{1,0:T(8,128)S(1)} %get-tuple-element.49), channel_id=1, source_target_pairs={{0,8},{1,9},{2,10},{3,11},{4,12},{5,13},{6,14},{7,15},{8,0},{9,1},... | collective-permute-start | bytes 1228808 | tf_op jit(solution)/shard_map/ppermute | solution.py:36
  207.0 7.3 %collective-permute-start.55 = (f32[32,128]{1,0:T(8,128)S(1)}, f32[32,128]{1,0:T(8,128)S(1)}, u32[]{:S(2)}, u32[]{:S(2)}) collective-permute-start(f32[32,128]{1,0:T(8,128)S(1)} %add.61), channel_id=1, source_target_pairs={{0,12},{1,13},{2,14},{3,15},{4,8},{5,9},{6,10},{7,11},{8,4},{9,5},... | collective-permute-start | bytes 49160 | tf_op jit(solution)/shard_map/ppermute | solution.py:36
  (25 other events, 119.3 us)

commit v2 on v1

--- a/solution.py
+++ b/solution.py
@@ -187,24 +187,51 @@
     lax.fori_loop(0, wide.shape[1] // block, add, 0)
 
 
+def place_pieces(order, step, pieces, spots, panel, half):
+    for piece, spot in zip(pieces, spots):
+        base = step * XY_COUNT + spot
+
+        def place(k, carry, piece=piece, base=base):
+            source = pl.multiple_of(k * half, half)
+            start = pl.multiple_of(order[base + k] * half, half)
+            panel[pl.ds(start, half), :] = piece[pl.ds(source, half), :]
+            return carry
+
+        lax.fori_loop(0, piece.shape[0] // half, place, 0)
+
+
+EARLY = (0, 2, 4)
+EARLY_SPOTS = (0, 16, 32)
+LATE = (1, 3, 5, 6)
+LATE_SPOTS = (8, 24, 48, 56)
+
+
+def place_body(step, half, order, *refs):
+    place_pieces(order, step, refs[:-1], EARLY_SPOTS, refs[-1], half)
+
+
+def place_early(step, order, pieces, half, full):
+    cols = pieces[0].shape[1]
+    return pl.pallas_call(
+        functools.partial(place_body, step, half),
+        out_shape=jax.ShapeDtypeStruct((full, cols), jnp.bfloat16),
+        in_specs=[smem()] + [vmem()] * len(pieces),
+        out_specs=vmem(),
+        name="place_early",
+        compiler_params=pltpu.CompilerParams(vmem_limit_bytes=14 * 2**20),
+        cost_estimate=pl.CostEstimate(
+            flops=2**28, bytes_accessed=full * cols, transcendentals=0
+        ),
+    )(order, *pieces)
+
+
 def first_body(step, n_right, n_left, order, *refs):
     right = refs[:n_right]
     left = refs[n_right : n_right + n_left]
-    top, bottom, panel, wide, summed = refs[n_right + n_left :]
+    top, bottom, panel, wide, summed = refs[n_right + n_left + 1 :]
     rows, cols = summed.shape
     half = rows // 2
-    spot = step * XY_COUNT
-    for piece in right:
-        count = piece.shape[0] // half
-
-        def place(k, carry, piece=piece, spot=spot):
-            source = pl.multiple_of(k * half, half)
-            start = pl.multiple_of(order[spot + k] * half, half)
-            panel[pl.ds(start, half), :] = piece[pl.ds(source, half), :]
-            return carry
-
-        lax.fori_loop(0, count, place, 0)
-        spot += count
+    place_pieces(order, step, right, LATE_SPOTS, panel, half)
     lay_rows(order, left, wide, 0, rows)
     multiply(wide, panel, summed)
     top[:half, :] = summed[:half, :].astype(jnp.bfloat16)
@@ -231,10 +258,13 @@
         jax.ShapeDtypeStruct((half, cols), jnp.bfloat16),
         jax.ShapeDtypeStruct((full, cols), jnp.bfloat16),
     ]
+    started = place_early(step, order, [right[k] for k in EARLY], half, full)
+    right = [right[k] for k in LATE]
     return pl.pallas_call(
         functools.partial(first_body, step, len(right), len(left)),
         out_shape=shapes,
-        in_specs=[smem()] + [vmem()] * (len(right) + len(left)),
+        in_specs=[smem()] + [vmem()] * (len(right) + len(left) + 1),
+        input_output_aliases={1 + len(right) + len(left): 2},
         out_specs=[vmem()] * len(shapes),
         scratch_shapes=[
             pltpu.VMEM((rows, full), jnp.bfloat16),
@@ -245,7 +275,7 @@
         cost_estimate=pl.CostEstimate(
             flops=2 * rows * cols * full, bytes_accessed=2 * full * cols, transcendentals=0
         ),
-    )(order, *right, *left)
+    )(order, *right, *left, started)
 
 
 def second_body(step, part, order, shift, panel, current, *refs):

time: 219 us -> 219 us (level)
  starting transfers between devices: 84.7 us -> 80.8 us
  waiting for transfers between devices: 102 us -> 105 us
    ppermute x56, starting transfers between devices: 84.7 us -> 80.8 us  [permute(): lax.ppermute(value, AXES, [(rank(*d), rank(*target(*d))) for d in EVERY])]
    ppermute x56, waiting for transfers between devices: 102 us -> 105 us  [permute(): lax.ppermute(value, AXES, [(rank(*d), rank(*target(*d))) for d in EVERY])]
  transfers between devices with their start and end apart: 56 -> 56, of which waited for: 36 -> 36; matrix products, arithmetic and copies ran while one was open for 4% -> 4% of each run, Pallas kernels for 3% -> 4%
where the time goes in v2:
time: 219 us; the launch traced here: 216 us
  waiting for transfers between devices  105 us (48%)
  starting transfers between devices  80.8 us (37%)
  Pallas kernels  19.3 us (9%)
  local copies, waits for them, and re-layouts  8.86 us (4%)
    ppermute x56, waiting for transfers between devices, permute(): lax.ppermute(value, AXES, [(rank(*d), rank(*target(*d))) for d in EVERY])  105 us
    ppermute x56, starting transfers between devices, permute(): lax.ppermute(value, AXES, [(rank(*d), rank(*target(*d))) for d in EVERY])  80.8 us
    pallas_call x4, Pallas kernels, second_product(): pl.pallas_call(functools.partial(second_body, step, part), out_shape=shap...  9.85 us
    pallas_call x2, Pallas kernels, first_product(): pl.pallas_call(functools.partial(first_body, step, len(right), len(left))...  7.33 us
    unnamed x22, local copies, waits for them, and re-layouts  6.3 us
  transfers between devices with their start and end apart: 56, of which 36 were waited for; matrix products, arithmetic and copies ran while one was open for 4% of the time, Pallas kernels for 4%

profile of v2, /device:TPU:32, one launch (start us, length us, event | category | flops | bytes accessed | tf_op | source)
XLA Modules:
  0.0 216.0 jit_solution(7390275652306211616)
XLA Ops:
  9.4 2.9 %collective-permute-done.2 = bf16[160,640]{1,0:T(8,128)(2,1)S(1)} collective-permute-done((bf16[160,640]{1,0:T(8,128)(2,1)S(1)}, bf16[160,640]{1,0:T(8,128)(2,1)S(1)}, u32[]{:S(2)}, u32[]{:S(2)}) %collective-permute-start.2) | collective-permute-done | bytes 204832 | tf_op jit(solution)/shard_map/ppermute | solution.py:36
  29.6 3.6 %collective-permute-done.11 = bf16[160,640]{1,0:T(8,128)(2,1)S(1)} collective-permute-done((bf16[160,640]{1,0:T(8,128)(2,1)S(1)}, bf16[160,640]{1,0:T(8,128)(2,1)S(1)}, u32[]{:S(2)}, u32[]{:S(2)}) %collective-permute-start.11) | collective-permute-done | bytes 204832 | tf_op jit(solution)/shard_map/ppermute | solution.py:36
  33.3 4.3 %collective-permute-start.12 = (bf16[320,640]{1,0:T(8,128)(2,1)S(1)}, bf16[320,640]{1,0:T(8,128)(2,1)S(1)}, u32[]{:S(2)}, u32[]{:S(2)}) collective-permute-start(bf16[320,640]{1,0:T(8,128)(2,1)S(1)} %constant_dynamic-update-slice_fusion.8.refs_4_), channel_id=1, source_target_pairs={{0,15},{1,8},{2,9},{3,10},{4,11},{5,12},{6,13},{7,14},{8,1},{9,2},... | collective-permute-start | bytes 1228808 | tf_op jit(solution)/shard_map/ppermute | solution.py:36
  37.6 5.6 %collective-permute-done.12.refs_5_ = bf16[320,640]{1,0:T(8,128)(2,1)S(1)} collective-permute-done((bf16[320,640]{1,0:T(8,128)(2,1)S(1)}, bf16[320,640]{1,0:T(8,128)(2,1)S(1)}, u32[]{:S(2)}, u32[]{:S(2)}) %collective-permute-start.12) | collective-permute-done | bytes 409632 | tf_op jit(solution)/shard_map/ppermute | solution.py:36
  45.1 5.5 %collective-permute-done.13.refs_6_ = bf16[320,640]{1,0:T(8,128)(2,1)S(1)} collective-permute-done((bf16[320,640]{1,0:T(8,128)(2,1)S(1)}, bf16[320,640]{1,0:T(8,128)(2,1)S(1)}, u32[]{:S(2)}, u32[]{:S(2)}) %collective-permute-start.13) | collective-permute-done | bytes 409632 | tf_op jit(solution)/shard_map/ppermute | solution.py:36
  50.6 3.0 %collective-permute-start.14 = (bf16[320,640]{1,0:T(8,128)(2,1)S(1)}, bf16[320,640]{1,0:T(8,128)(2,1)S(1)}, u32[]{:S(2)}, u32[]{:S(2)}) collective-permute-start(bf16[320,640]{1,0:T(8,128)(2,1)S(1)} %collective-permute-done.13.refs_6_), channel_id=1, source_target_pairs={{0,15},{1,8},{2,9},{3,10},{4,11},{5,12},{6,13},{7,14},{8,1},{9,2},... | collective-permute-start | bytes 1228808 | tf_op jit(solution)/shard_map/ppermute | solution.py:36
  54.6 4.6 %collective-permute-done.14.refs_7_ = bf16[320,640]{1,0:T(8,128)(2,1)S(1)} collective-permute-done((bf16[320,640]{1,0:T(8,128)(2,1)S(1)}, bf16[320,640]{1,0:T(8,128)(2,1)S(1)}, u32[]{:S(2)}, u32[]{:S(2)}) %collective-permute-start.14) | collective-permute-done | bytes 409632 | tf_op jit(solution)/shard_map/ppermute | solution.py:36
  59.2 4.1 %first_product.2 = (bf16[96,640]{1,0:T(8,128)(2,1)S(1)}, bf16[80,640]{1,0:T(8,128)(2,1)S(1)}, bf16[5120,640]{1,0:T(8,128)(2,1)S(1)}) custom-call(s32[136]{0:T(256)S(1)} %bitcast.3, bf16[640,640]{1,0:T(8,128)(2,1)S(1)} %collective-permute-done.4.refs_0_, bf16[640,640]{1,0:T(8,128)(2,1)S(1)} %collective-permute-done.8.refs_1_, ...), custom_call_target="tpu_custom_call", output_to_operand_aliasing={{2}: (9, {})} | custom-call | flops 1048576000 | bytes 6553600 | tf_op jit(solution)/shard_map/first_product/pallas_call | solution.py:263
  67.7 3.0 %collective-permute-start.17 = (bf16[192,640]{1,0:T(8,128)(2,1)S(1)}, bf16[192,640]{1,0:T(8,128)(2,1)S(1)}, u32[]{:S(2)}, u32[]{:S(2)}) collective-permute-start(bf16[192,640]{1,0:T(8,128)(2,1)S(1)} %constant_dynamic-update-slice_fusion.18.refs_0_), channel_id=1, source_target_pairs={{0,15},{1,8},{2,9},{3,10},{4,11},{5,12},{6,13},{7,14},{8,1},{9,2},... | collective-permute-start | bytes 737288 | tf_op jit(solution)/shard_map/ppermute | solution.py:36
  70.8 2.6 %collective-permute-start.25 = (bf16[160,640]{1,0:T(8,128)(2,1)S(1)}, bf16[160,640]{1,0:T(8,128)(2,1)S(1)}, u32[]{:S(2)}, u32[]{:S(2)}) collective-permute-start(bf16[160,640]{1,0:T(8,128)(2,1)S(1)} %constant_dynamic-update-slice_fusion.24.refs_0_), channel_id=1, source_target_pairs={{0,15},{1,8},{2,9},{3,10},{4,11},{5,12},{6,13},{7,14},{8,1},{9,2},... | collective-permute-start | bytes 614408 | tf_op jit(solution)/shard_map/ppermute | solution.py:36
  80.3 3.1 %collective-permute-start.19 = (bf16[192,640]{1,0:T(8,128)(2,1)S(1)}, bf16[192,640]{1,0:T(8,128)(2,1)S(1)}, u32[]{:S(2)}, u32[]{:S(2)}) collective-permute-start(bf16[192,640]{1,0:T(8,128)(2,1)S(1)} %collective-permute-done.18.refs_2_), channel_id=1, source_target_pairs={{0,15},{1,8},{2,9},{3,10},{4,11},{5,12},{6,13},{7,14},{8,1},{9,2},... | collective-permute-start | bytes 737288 | tf_op jit(solution)/shard_map/ppermute | solution.py:36
  103.2 4.5 %collective-permute-start.30 = (bf16[320,640]{1,0:T(8,128)(2,1)S(1)}, bf16[320,640]{1,0:T(8,128)(2,1)S(1)}, u32[]{:S(2)}, u32[]{:S(2)}) collective-permute-start(bf16[320,640]{1,0:T(8,128)(2,1)S(1)} %pad_maximum_fusion.3), channel_id=1, source_target_pairs={{0,56},{1,57},{2,58},{3,59},{4,60},{5,61},{6,62},{7,63},{8,192},{9... | collective-permute-start | bytes 1228808 | tf_op jit(solution)/shard_map/ppermute | solution.py:36
  109.2 4.2 %collective-permute-done.30 = bf16[320,640]{1,0:T(8,128)(2,1)S(1)} collective-permute-done((bf16[320,640]{1,0:T(8,128)(2,1)S(1)}, bf16[320,640]{1,0:T(8,128)(2,1)S(1)}, u32[]{:S(2)}, u32[]{:S(2)}) %collective-permute-start.30) | collective-permute-done | bytes 409632 | tf_op jit(solution)/shard_map/ppermute | solution.py:36
  116.7 5.2 %collective-permute-done.34 = bf16[160,640]{1,0:T(8,128)(2,1)S(1)} collective-permute-done((bf16[160,640]{1,0:T(8,128)(2,1)S(1)}, bf16[160,640]{1,0:T(8,128)(2,1)S(1)}, u32[]{:S(2)}, u32[]{:S(2)}) %collective-permute-start.34) | collective-permute-done | bytes 204832 | tf_op jit(solution)/shard_map/ppermute | solution.py:36
  121.9 3.3 %collective-permute-start.35 = (bf16[320,640]{1,0:T(8,128)(2,1)S(1)}, bf16[320,640]{1,0:T(8,128)(2,1)S(1)}, u32[]{:S(2)}, u32[]{:S(2)}) collective-permute-start(bf16[320,640]{1,0:T(8,128)(2,1)S(1)} %constant_dynamic-update-slice_fusion.30.refs_4_), channel_id=1, source_target_pairs={{0,15},{1,8},{2,9},{3,10},{4,11},{5,12},{6,13},{7,14},{8,1},{9,2},... | collective-permute-start | bytes 1228808 | tf_op jit(solution)/shard_map/ppermute | solution.py:36
  125.2 5.6 %collective-permute-done.35.refs_5_ = bf16[320,640]{1,0:T(8,128)(2,1)S(1)} collective-permute-done((bf16[320,640]{1,0:T(8,128)(2,1)S(1)}, bf16[320,640]{1,0:T(8,128)(2,1)S(1)}, u32[]{:S(2)}, u32[]{:S(2)}) %collective-permute-start.35) | collective-permute-done | bytes 409632 | tf_op jit(solution)/shard_map/ppermute | solution.py:36
  133.1 5.1 %collective-permute-done.36.refs_6_ = bf16[320,640]{1,0:T(8,128)(2,1)S(1)} collective-permute-done((bf16[320,640]{1,0:T(8,128)(2,1)S(1)}, bf16[320,640]{1,0:T(8,128)(2,1)S(1)}, u32[]{:S(2)}, u32[]{:S(2)}) %collective-permute-start.36) | collective-permute-done | bytes 409632 | tf_op jit(solution)/shard_map/ppermute | solution.py:36
  138.2 3.0 %collective-permute-start.37 = (bf16[320,640]{1,0:T(8,128)(2,1)S(1)}, bf16[320,640]{1,0:T(8,128)(2,1)S(1)}, u32[]{:S(2)}, u32[]{:S(2)}) collective-permute-start(bf16[320,640]{1,0:T(8,128)(2,1)S(1)} %collective-permute-done.36.refs_6_), channel_id=1, source_target_pairs={{0,15},{1,8},{2,9},{3,10},{4,11},{5,12},{6,13},{7,14},{8,1},{9,2},... | collective-permute-start | bytes 1228808 | tf_op jit(solution)/shard_map/ppermute | solution.py:36
  142.3 4.6 %collective-permute-done.37.refs_7_ = bf16[320,640]{1,0:T(8,128)(2,1)S(1)} collective-permute-done((bf16[320,640]{1,0:T(8,128)(2,1)S(1)}, bf16[320,640]{1,0:T(8,128)(2,1)S(1)}, u32[]{:S(2)}, u32[]{:S(2)}) %collective-permute-start.37) | collective-permute-done | bytes 409632 | tf_op jit(solution)/shard_map/ppermute | solution.py:36
  146.9 3.2 %first_product.3 = (bf16[80,640]{1,0:T(8,128)(2,1)S(1)}, bf16[80,640]{1,0:T(8,128)(2,1)S(1)}, bf16[5120,640]{1,0:T(8,128)(2,1)S(1)}) custom-call(s32[136]{0:T(256)S(1)} %bitcast.7, bf16[640,640]{1,0:T(8,128)(2,1)S(1)} %collective-permute-done.23.refs_0_, bf16[640,640]{1,0:T(8,128)(2,1)S(1)} %collective-permute-done.31.refs_1_, ...), custom_call_target="tpu_custom_call", output_to_operand_aliasing={{2}: (9, {})} | custom-call | flops 1048576000 | bytes 6553600 | tf_op jit(solution)/shard_map/first_product/pallas_call | solution.py:263
  152.0 3.3 %collective-permute-done.43 = bf16[80,640]{1,0:T(8,128)(2,1)S(1)} collective-permute-done((bf16[80,640]{1,0:T(8,128)(2,1)S(1)}, bf16[80,640]{1,0:T(8,128)(2,1)S(1)}, u32[]{:S(2)}, u32[]{:S(2)}) %collective-permute-start.43) | collective-permute-done | bytes 102432 | tf_op jit(solution)/shard_map/ppermute | solution.py:36
  155.4 4.6 %collective-permute-start.44 = (bf16[160,640]{1,0:T(8,128)(2,1)S(1)}, bf16[160,640]{1,0:T(8,128)(2,1)S(1)}, u32[]{:S(2)}, u32[]{:S(2)}) collective-permute-start(bf16[160,640]{1,0:T(8,128)(2,1)S(1)} %constant_dynamic-update-slice_fusion.42.refs_0_), channel_id=1, source_target_pairs={{0,15},{1,8},{2,9},{3,10},{4,11},{5,12},{6,13},{7,14},{8,1},{9,2},... | collective-permute-start | bytes 614408 | tf_op jit(solution)/shard_map/ppermute | solution.py:36
  160.1 3.3 %collective-permute-done.44.refs_1_ = bf16[160,640]{1,0:T(8,128)(2,1)S(1)} collective-permute-done((bf16[160,640]{1,0:T(8,128)(2,1)S(1)}, bf16[160,640]{1,0:T(8,128)(2,1)S(1)}, u32[]{:S(2)}, u32[]{:S(2)}) %collective-permute-start.44) | collective-permute-done | bytes 204832 | tf_op jit(solution)/shard_map/ppermute | solution.py:36
  163.8 2.7 %collective-permute-done.40.refs_1_ = bf16[160,640]{1,0:T(8,128)(2,1)S(1)} collective-permute-done((bf16[160,640]{1,0:T(8,128)(2,1)S(1)}, bf16[160,640]{1,0:T(8,128)(2,1)S(1)}, u32[]{:S(2)}, u32[]{:S(2)}) %collective-permute-start.40) | collective-permute-done | bytes 204832 | tf_op jit(solution)/shard_map/ppermute | solution.py:36
  168.6 3.2 %collective-permute-start.46 = (bf16[160,640]{1,0:T(8,128)(2,1)S(1)}, bf16[160,640]{1,0:T(8,128)(2,1)S(1)}, u32[]{:S(2)}, u32[]{:S(2)}) collective-permute-start(bf16[160,640]{1,0:T(8,128)(2,1)S(1)} %collective-permute-done.45.refs_2_), channel_id=1, source_target_pairs={{0,15},{1,8},{2,9},{3,10},{4,11},{5,12},{6,13},{7,14},{8,1},{9,2},... | collective-permute-start | bytes 614408 | tf_op jit(solution)/shard_map/ppermute | solution.py:36
  172.4 4.5 %collective-permute-start.42 = (bf16[160,640]{1,0:T(8,128)(2,1)S(1)}, bf16[160,640]{1,0:T(8,128)(2,1)S(1)}, u32[]{:S(2)}, u32[]{:S(2)}) collective-permute-start(bf16[160,640]{1,0:T(8,128)(2,1)S(1)} %collective-permute-done.41.refs_2_), channel_id=1, source_target_pairs={{0,15},{1,8},{2,9},{3,10},{4,11},{5,12},{6,13},{7,14},{8,1},{9,2},... | collective-permute-start | bytes 614408 | tf_op jit(solution)/shard_map/ppermute | solution.py:36
  185.0 2.8 %collective-permute-done.49 = f32[32,128]{1,0:T(8,128)S(1)} collective-permute-done((f32[32,128]{1,0:T(8,128)S(1)}, f32[32,128]{1,0:T(8,128)S(1)}, u32[]{:S(2)}, u32[]{:S(2)}) %collective-permute-start.49) | collective-permute-done | bytes 16416 | tf_op jit(solution)/shard_map/ppermute | solution.py:36
  187.7 4.4 %collective-permute-done.50 = f32[32,128]{1,0:T(8,128)S(1)} collective-permute-done((f32[32,128]{1,0:T(8,128)S(1)}, f32[32,128]{1,0:T(8,128)S(1)}, u32[]{:S(2)}, u32[]{:S(2)}) %collective-permute-start.50) | collective-permute-done | bytes 16416 | tf_op jit(solution)/shard_map/ppermute | solution.py:36
  192.1 3.2 %collective-permute-done.51 = f32[32,128]{1,0:T(8,128)S(1)} collective-permute-done((f32[32,128]{1,0:T(8,128)S(1)}, f32[32,128]{1,0:T(8,128)S(1)}, u32[]{:S(2)}, u32[]{:S(2)}) %collective-permute-start.51) | collective-permute-done | bytes 16416 | tf_op jit(solution)/shard_map/ppermute | solution.py:36
  195.3 4.4 %collective-permute-done.52 = f32[32,128]{1,0:T(8,128)S(1)} collective-permute-done((f32[32,128]{1,0:T(8,128)S(1)}, f32[32,128]{1,0:T(8,128)S(1)}, u32[]{:S(2)}, u32[]{:S(2)}) %collective-permute-start.52) | collective-permute-done | bytes 16416 | tf_op jit(solution)/shard_map/ppermute | solution.py:36
  202.9 4.1 %collective-permute-done.54 = f32[32,128]{1,0:T(8,128)S(1)} collective-permute-done((f32[32,128]{1,0:T(8,128)S(1)}, f32[32,128]{1,0:T(8,128)S(1)}, u32[]{:S(2)}, u32[]{:S(2)}) %collective-permute-start.54) | collective-permute-done | bytes 16416 | tf_op jit(solution)/shard_map/ppermute | solution.py:36
  208.8 5.3 %collective-permute-done.55 = f32[32,128]{1,0:T(8,128)S(1)} collective-permute-done((f32[32,128]{1,0:T(8,128)S(1)}, f32[32,128]{1,0:T(8,128)S(1)}, u32[]{:S(2)}, u32[]{:S(2)}) %collective-permute-start.55) | collective-permute-done | bytes 16416 | tf_op jit(solution)/shard_map/ppermute | solution.py:36
  (141 shorter events, 88.2 us)
Async XLA Ops:
  5.1 22.9 %collective-permute-start = (bf16[160,640]{1,0:T(8,128)(2,1)S(1)}, bf16[160,640]{1,0:T(8,128)(2,1)S(1)}, u32[]{:S(2)}, u32[]{:S(2)}) collective-permute-start(bf16[160,640]{1,0:T(8,128)(2,1)S(1)} %get-tuple-element.27), channel_id=1, source_target_pairs={{0,8},{1,9},{2,10},{3,11},{4,12},{5,13},{6,14},{7,15},{8,0},{9,1},... | collective-permute-start | bytes 614408 | tf_op jit(solution)/shard_map/ppermute | solution.py:36
  12.4 7.5 %collective-permute-start.3 = (bf16[320,640]{1,0:T(8,128)(2,1)S(1)}, bf16[320,640]{1,0:T(8,128)(2,1)S(1)}, u32[]{:S(2)}, u32[]{:S(2)}) collective-permute-start(bf16[320,640]{1,0:T(8,128)(2,1)S(1)} %pad_maximum_fusion), channel_id=1, source_target_pairs={{0,24},{1,25},{2,26},{3,27},{4,28},{5,29},{6,30},{7,31},{8,64},{9,... | collective-permute-start | bytes 1228808 | tf_op jit(solution)/shard_map/ppermute | solution.py:36
  15.2 8.7 %collective-permute-start.7 = (bf16[320,640]{1,0:T(8,128)(2,1)S(1)}, bf16[320,640]{1,0:T(8,128)(2,1)S(1)}, u32[]{:S(2)}, u32[]{:S(2)}) collective-permute-start(bf16[320,640]{1,0:T(8,128)(2,1)S(1)} %pad_maximum_fusion.1), channel_id=1, source_target_pairs={{0,56},{1,57},{2,58},{3,59},{4,60},{5,61},{6,62},{7,63},{8,192},{9... | collective-permute-start | bytes 1228808 | tf_op jit(solution)/shard_map/ppermute | solution.py:36
  24.7 19.0 %collective-permute-start.8 = (bf16[640,640]{1,0:T(8,128)(2,1)S(1)}, bf16[640,640]{1,0:T(8,128)(2,1)S(1)}, u32[]{:S(2)}, u32[]{:S(2)}) collective-permute-start(bf16[640,640]{1,0:T(8,128)(2,1)S(1)} %get-tuple-element.58.refs_1_), channel_id=1, source_target_pairs={{0,24},{1,25},{2,26},{3,27},{4,28},{5,29},{6,30},{7,31},{8,64},{9,... | collective-permute-start | bytes 2457608 | tf_op jit(solution)/shard_map/ppermute | solution.py:36
  25.3 19.7 %collective-permute-start.4 = (bf16[640,640]{1,0:T(8,128)(2,1)S(1)}, bf16[640,640]{1,0:T(8,128)(2,1)S(1)}, u32[]{:S(2)}, u32[]{:S(2)}) collective-permute-start(bf16[640,640]{1,0:T(8,128)(2,1)S(1)} %get-tuple-element.60.refs_0_), channel_id=1, source_target_pairs={{0,56},{1,57},{2,58},{3,59},{4,60},{5,61},{6,62},{7,63},{8,192},{9... | collective-permute-start | bytes 2457608 | tf_op jit(solution)/shard_map/ppermute | solution.py:36
  27.2 26.3 %collective-permute-start.15 = (bf16[1280,640]{1,0:T(8,128)(2,1)}, bf16[1280,640]{1,0:T(8,128)(2,1)S(1)}, u32[]{:S(2)}, u32[]{:S(2)}) collective-permute-start(bf16[1280,640]{1,0:T(8,128)(2,1)} %get-tuple-element.57), channel_id=1, source_target_pairs={{0,8},{1,9},{2,10},{3,11},{4,12},{5,13},{6,14},{7,15},{8,0},{9,1},... | collective-permute-start | bytes 4915208 | tf_op jit(solution)/shard_map/ppermute | solution.py:36
  33.3 10.0 %collective-permute-start.12 = (bf16[320,640]{1,0:T(8,128)(2,1)S(1)}, bf16[320,640]{1,0:T(8,128)(2,1)S(1)}, u32[]{:S(2)}, u32[]{:S(2)}) collective-permute-start(bf16[320,640]{1,0:T(8,128)(2,1)S(1)} %constant_dynamic-update-slice_fusion.8.refs_4_), channel_id=1, source_target_pairs={{0,15},{1,8},{2,9},{3,10},{4,11},{5,12},{6,13},{7,14},{8,1},{9,2},... | collective-permute-start | bytes 1228808 | tf_op jit(solution)/shard_map/ppermute | solution.py:36
  43.2 7.4 %collective-permute-start.13 = (bf16[320,640]{1,0:T(8,128)(2,1)S(1)}, bf16[320,640]{1,0:T(8,128)(2,1)S(1)}, u32[]{:S(2)}, u32[]{:S(2)}) collective-permute-start(bf16[320,640]{1,0:T(8,128)(2,1)S(1)} %collective-permute-done.12.refs_5_), channel_id=1, source_target_pairs={{0,9},{1,10},{2,11},{3,12},{4,13},{5,14},{6,15},{7,8},{8,7},{9,0},... | collective-permute-start | bytes 1228808 | tf_op jit(solution)/shard_map/ppermute | solution.py:36
  43.7 15.4 %collective-permute-start.10 = (bf16[640,640]{1,0:T(8,128)(2,1)S(1)}, bf16[640,640]{1,0:T(8,128)(2,1)S(1)}, u32[]{:S(2)}, u32[]{:S(2)}) collective-permute-start(bf16[640,640]{1,0:T(8,128)(2,1)S(1)} %collective-permute-done.8.refs_1_), channel_id=1, source_target_pairs={{0,8},{1,9},{2,10},{3,11},{4,12},{5,13},{6,14},{7,15},{8,0},{9,1},... | collective-permute-start | bytes 2457608 | tf_op jit(solution)/shard_map/ppermute | solution.py:36
  45.0 14.2 %collective-permute-start.9 = (bf16[640,640]{1,0:T(8,128)(2,1)S(1)}, bf16[640,640]{1,0:T(8,128)(2,1)S(1)}, u32[]{:S(2)}, u32[]{:S(2)}) collective-permute-start(bf16[640,640]{1,0:T(8,128)(2,1)S(1)} %collective-permute-done.4.refs_0_), channel_id=1, source_target_pairs={{0,8},{1,9},{2,10},{3,11},{4,12},{5,13},{6,14},{7,15},{8,0},{9,1},... | collective-permute-start | bytes 2457608 | tf_op jit(solution)/shard_map/ppermute | solution.py:36
  50.6 8.6 %collective-permute-start.14 = (bf16[320,640]{1,0:T(8,128)(2,1)S(1)}, bf16[320,640]{1,0:T(8,128)(2,1)S(1)}, u32[]{:S(2)}, u32[]{:S(2)}) collective-permute-start(bf16[320,640]{1,0:T(8,128)(2,1)S(1)} %collective-permute-done.13.refs_6_), channel_id=1, source_target_pairs={{0,15},{1,8},{2,9},{3,10},{4,11},{5,12},{6,13},{7,14},{8,1},{9,2},... | collective-permute-start | bytes 1228808 | tf_op jit(solution)/shard_map/ppermute | solution.py:36
  64.0 6.8 %collective-permute-start.24 = (bf16[80,640]{1,0:T(8,128)(2,1)S(1)}, bf16[80,640]{1,0:T(8,128)(2,1)S(1)}, u32[]{:S(2)}, u32[]{:S(2)}) collective-permute-start(bf16[80,640]{1,0:T(8,128)(2,1)S(1)} %get-tuple-element.36), channel_id=1, source_target_pairs={{0,9},{1,10},{2,11},{3,12},{4,13},{5,14},{6,15},{7,8},{8,7},{9,0},... | collective-permute-start | bytes 307208 | tf_op jit(solution)/shard_map/ppermute | solution.py:36
  67.7 6.9 %collective-permute-start.17 = (bf16[192,640]{1,0:T(8,128)(2,1)S(1)}, bf16[192,640]{1,0:T(8,128)(2,1)S(1)}, u32[]{:S(2)}, u32[]{:S(2)}) collective-permute-start(bf16[192,640]{1,0:T(8,128)(2,1)S(1)} %constant_dynamic-update-slice_fusion.18.refs_0_), channel_id=1, source_target_pairs={{0,15},{1,8},{2,9},{3,10},{4,11},{5,12},{6,13},{7,14},{8,1},{9,2},... | collective-permute-start | bytes 737288 | tf_op jit(solution)/shard_map/ppermute | solution.py:36
  76.8 6.6 %collective-permute-start.26 = (bf16[160,640]{1,0:T(8,128)(2,1)S(1)}, bf16[160,640]{1,0:T(8,128)(2,1)S(1)}, u32[]{:S(2)}, u32[]{:S(2)}) collective-permute-start(bf16[160,640]{1,0:T(8,128)(2,1)S(1)} %collective-permute-done.25.refs_1_), channel_id=1, source_target_pairs={{0,9},{1,10},{2,11},{3,12},{4,13},{5,14},{6,15},{7,8},{8,7},{9,0},... | collective-permute-start | bytes 614408 | tf_op jit(solution)/shard_map/ppermute | solution.py:36
  80.3 7.0 %collective-permute-start.19 = (bf16[192,640]{1,0:T(8,128)(2,1)S(1)}, bf16[192,640]{1,0:T(8,128)(2,1)S(1)}, u32[]{:S(2)}, u32[]{:S(2)}) collective-permute-start(bf16[192,640]{1,0:T(8,128)(2,1)S(1)} %collective-permute-done.18.refs_2_), channel_id=1, source_target_pairs={{0,15},{1,8},{2,9},{3,10},{4,11},{5,12},{6,13},{7,14},{8,1},{9,2},... | collective-permute-start | bytes 737288 | tf_op jit(solution)/shard_map/ppermute | solution.py:36
  83.4 6.6 %collective-permute-start.27 = (bf16[160,640]{1,0:T(8,128)(2,1)S(1)}, bf16[160,640]{1,0:T(8,128)(2,1)S(1)}, u32[]{:S(2)}, u32[]{:S(2)}) collective-permute-start(bf16[160,640]{1,0:T(8,128)(2,1)S(1)} %collective-permute-done.26.refs_2_), channel_id=1, source_target_pairs={{0,15},{1,8},{2,9},{3,10},{4,11},{5,12},{6,13},{7,14},{8,1},{9,2},... | collective-permute-start | bytes 614408 | tf_op jit(solution)/shard_map/ppermute | solution.py:36
  100.8 8.1 %collective-permute-start.22 = (bf16[320,640]{1,0:T(8,128)(2,1)S(1)}, bf16[320,640]{1,0:T(8,128)(2,1)S(1)}, u32[]{:S(2)}, u32[]{:S(2)}) collective-permute-start(bf16[320,640]{1,0:T(8,128)(2,1)S(1)} %pad_maximum_fusion.2), channel_id=1, source_target_pairs={{0,24},{1,25},{2,26},{3,27},{4,28},{5,29},{6,30},{7,31},{8,64},{9,... | collective-permute-start | bytes 1228808 | tf_op jit(solution)/shard_map/ppermute | solution.py:36
  103.2 10.2 %collective-permute-start.30 = (bf16[320,640]{1,0:T(8,128)(2,1)S(1)}, bf16[320,640]{1,0:T(8,128)(2,1)S(1)}, u32[]{:S(2)}, u32[]{:S(2)}) collective-permute-start(bf16[320,640]{1,0:T(8,128)(2,1)S(1)} %pad_maximum_fusion.3), channel_id=1, source_target_pairs={{0,56},{1,57},{2,58},{3,59},{4,60},{5,61},{6,62},{7,63},{8,192},{9... | collective-permute-start | bytes 1228808 | tf_op jit(solution)/shard_map/ppermute | solution.py:36
  113.5 27.8 %collective-permute-start.38 = (bf16[1280,640]{1,0:T(8,128)(2,1)S(1)}, bf16[1280,640]{1,0:T(8,128)(2,1)S(1)}, u32[]{:S(2)}, u32[]{:S(2)}) collective-permute-start(bf16[1280,640]{1,0:T(8,128)(2,1)S(1)} %get-tuple-element.53), channel_id=1, source_target_pairs={{0,8},{1,9},{2,10},{3,11},{4,12},{5,13},{6,14},{7,15},{8,0},{9,1},... | collective-permute-start | bytes 4915208 | tf_op jit(solution)/shard_map/ppermute | solution.py:36
  114.2 17.1 %collective-permute-start.31 = (bf16[640,640]{1,0:T(8,128)(2,1)S(1)}, bf16[640,640]{1,0:T(8,128)(2,1)S(1)}, u32[]{:S(2)}, u32[]{:S(2)}) collective-permute-start(bf16[640,640]{1,0:T(8,128)(2,1)S(1)} %get-tuple-element.54.refs_1_), channel_id=1, source_target_pairs={{0,24},{1,25},{2,26},{3,27},{4,28},{5,29},{6,30},{7,31},{8,64},{9,... | collective-permute-start | bytes 2457608 | tf_op jit(solution)/shard_map/ppermute | solution.py:36
  114.2 18.8 %collective-permute-start.23 = (bf16[640,640]{1,0:T(8,128)(2,1)S(1)}, bf16[640,640]{1,0:T(8,128)(2,1)S(1)}, u32[]{:S(2)}, u32[]{:S(2)}) collective-permute-start(bf16[640,640]{1,0:T(8,128)(2,1)S(1)} %get-tuple-element.56.refs_0_), channel_id=1, source_target_pairs={{0,56},{1,57},{2,58},{3,59},{4,60},{5,61},{6,62},{7,63},{8,192},{9... | collective-permute-start | bytes 2457608 | tf_op jit(solution)/shard_map/ppermute | solution.py:36
  121.9 8.9 %collective-permute-start.35 = (bf16[320,640]{1,0:T(8,128)(2,1)S(1)}, bf16[320,640]{1,0:T(8,128)(2,1)S(1)}, u32[]{:S(2)}, u32[]{:S(2)}) collective-permute-start(bf16[320,640]{1,0:T(8,128)(2,1)S(1)} %constant_dynamic-update-slice_fusion.30.refs_4_), channel_id=1, source_target_pairs={{0,15},{1,8},{2,9},{3,10},{4,11},{5,12},{6,13},{7,14},{8,1},{9,2},... | collective-permute-start | bytes 1228808 | tf_op jit(solution)/shard_map/ppermute | solution.py:36
  130.8 7.4 %collective-permute-start.36 = (bf16[320,640]{1,0:T(8,128)(2,1)S(1)}, bf16[320,640]{1,0:T(8,128)(2,1)S(1)}, u32[]{:S(2)}, u32[]{:S(2)}) collective-permute-start(bf16[320,640]{1,0:T(8,128)(2,1)S(1)} %collective-permute-done.35.refs_5_), channel_id=1, source_target_pairs={{0,9},{1,10},{2,11},{3,12},{4,13},{5,14},{6,15},{7,8},{8,7},{9,0},... | collective-permute-start | bytes 1228808 | tf_op jit(solution)/shard_map/ppermute | solution.py:36
  131.3 15.5 %collective-permute-start.33 = (bf16[640,640]{1,0:T(8,128)(2,1)S(1)}, bf16[640,640]{1,0:T(8,128)(2,1)S(1)}, u32[]{:S(2)}, u32[]{:S(2)}) collective-permute-start(bf16[640,640]{1,0:T(8,128)(2,1)S(1)} %collective-permute-done.31.refs_1_), channel_id=1, source_target_pairs={{0,8},{1,9},{2,10},{3,11},{4,12},{5,13},{6,14},{7,15},{8,0},{9,1},... | collective-permute-start | bytes 2457608 | tf_op jit(solution)/shard_map/ppermute | solution.py:36
  133.0 13.8 %collective-permute-start.32 = (bf16[640,640]{1,0:T(8,128)(2,1)S(1)}, bf16[640,640]{1,0:T(8,128)(2,1)S(1)}, u32[]{:S(2)}, u32[]{:S(2)}) collective-permute-start(bf16[640,640]{1,0:T(8,128)(2,1)S(1)} %collective-permute-done.23.refs_0_), channel_id=1, source_target_pairs={{0,8},{1,9},{2,10},{3,11},{4,12},{5,13},{6,14},{7,15},{8,0},{9,1},... | collective-permute-start | bytes 2457608 | tf_op jit(solution)/shard_map/ppermute | solution.py:36
  138.2 8.7 %collective-permute-start.37 = (bf16[320,640]{1,0:T(8,128)(2,1)S(1)}, bf16[320,640]{1,0:T(8,128)(2,1)S(1)}, u32[]{:S(2)}, u32[]{:S(2)}) collective-permute-start(bf16[320,640]{1,0:T(8,128)(2,1)S(1)} %collective-permute-done.36.refs_6_), channel_id=1, source_target_pairs={{0,15},{1,8},{2,9},{3,10},{4,11},{5,12},{6,13},{7,14},{8,1},{9,2},... | collective-permute-start | bytes 1228808 | tf_op jit(solution)/shard_map/ppermute | solution.py:36
  150.1 9.9 %collective-permute-start.39 = (bf16[80,640]{1,0:T(8,128)(2,1)S(1)}, bf16[80,640]{1,0:T(8,128)(2,1)S(1)}, u32[]{:S(2)}, u32[]{:S(2)}) collective-permute-start(bf16[80,640]{1,0:T(8,128)(2,1)S(1)} %get-tuple-element.43), channel_id=1, source_target_pairs={{0,9},{1,10},{2,11},{3,12},{4,13},{5,14},{6,15},{7,8},{8,7},{9,0},... | collective-permute-start | bytes 307208 | tf_op jit(solution)/shard_map/ppermute | solution.py:36
  155.4 8.1 %collective-permute-start.44 = (bf16[160,640]{1,0:T(8,128)(2,1)S(1)}, bf16[160,640]{1,0:T(8,128)(2,1)S(1)}, u32[]{:S(2)}, u32[]{:S(2)}) collective-permute-start(bf16[160,640]{1,0:T(8,128)(2,1)S(1)} %constant_dynamic-update-slice_fusion.42.refs_0_), channel_id=1, source_target_pairs={{0,15},{1,8},{2,9},{3,10},{4,11},{5,12},{6,13},{7,14},{8,1},{9,2},... | collective-permute-start | bytes 614408 | tf_op jit(solution)/shard_map/ppermute | solution.py:36
  168.6 8.2 %collective-permute-start.46 = (bf16[160,640]{1,0:T(8,128)(2,1)S(1)}, bf16[160,640]{1,0:T(8,128)(2,1)S(1)}, u32[]{:S(2)}, u32[]{:S(2)}) collective-permute-start(bf16[160,640]{1,0:T(8,128)(2,1)S(1)} %collective-permute-done.45.refs_2_), channel_id=1, source_target_pairs={{0,15},{1,8},{2,9},{3,10},{4,11},{5,12},{6,13},{7,14},{8,1},{9,2},... | collective-permute-start | bytes 614408 | tf_op jit(solution)/shard_map/ppermute | solution.py:36
  172.4 7.9 %collective-permute-start.42 = (bf16[160,640]{1,0:T(8,128)(2,1)S(1)}, bf16[160,640]{1,0:T(8,128)(2,1)S(1)}, u32[]{:S(2)}, u32[]{:S(2)}) collective-permute-start(bf16[160,640]{1,0:T(8,128)(2,1)S(1)} %collective-permute-done.41.refs_2_), channel_id=1, source_target_pairs={{0,15},{1,8},{2,9},{3,10},{4,11},{5,12},{6,13},{7,14},{8,1},{9,2},... | collective-permute-start | bytes 614408 | tf_op jit(solution)/shard_map/ppermute | solution.py:36
  182.7 32.5 %collective-permute-start.47 = (f32[160,640]{1,0:T(8,128)S(1)}, f32[160,640]{1,0:T(8,128)S(1)}, u32[]{:S(2)}, u32[]{:S(2)}) collective-permute-start(f32[160,640]{1,0:T(8,128)S(1)} %get-tuple-element.49), channel_id=1, source_target_pairs={{0,8},{1,9},{2,10},{3,11},{4,12},{5,13},{6,14},{7,15},{8,0},{9,1},... | collective-permute-start | bytes 1228808 | tf_op jit(solution)/shard_map/ppermute | solution.py:36
  206.9 7.2 %collective-permute-start.55 = (f32[32,128]{1,0:T(8,128)S(1)}, f32[32,128]{1,0:T(8,128)S(1)}, u32[]{:S(2)}, u32[]{:S(2)}) collective-permute-start(f32[32,128]{1,0:T(8,128)S(1)} %add.61), channel_id=1, source_target_pairs={{0,12},{1,13},{2,14},{3,15},{4,8},{5,9},{6,10},{7,11},{8,4},{9,5},... | collective-permute-start | bytes 49160 | tf_op jit(solution)/shard_map/ppermute | solution.py:36
  (25 other events, 118.5 us)

commit v3 on v2

--- a/solution.py
+++ b/solution.py
@@ -188,16 +188,25 @@
 
 
 def place_pieces(order, step, pieces, spots, panel, half):
+    total = jnp.zeros((8, panel.shape[1]), jnp.float32)
     for piece, spot in zip(pieces, spots):
         base = step * XY_COUNT + spot
 
         def place(k, carry, piece=piece, base=base):
             source = pl.multiple_of(k * half, half)
             start = pl.multiple_of(order[base + k] * half, half)
-            panel[pl.ds(start, half), :] = piece[pl.ds(source, half), :]
-            return carry
-
-        lax.fori_loop(0, piece.shape[0] // half, place, 0)
+            part = piece[pl.ds(source, half), :]
+            panel[pl.ds(start, half), :] = part
+            if step:
+                return carry
+            part = part.astype(jnp.float32)
+            return carry + fold_rows(part * part)
+
+        if step:
+            lax.fori_loop(0, piece.shape[0] // half, place, 0)
+        else:
+            total = lax.fori_loop(0, piece.shape[0] // half, place, total)
+    return total
 
 
 EARLY = (0, 2, 4)
@@ -207,16 +216,20 @@
 
 
 def place_body(step, half, order, *refs):
-    place_pieces(order, step, refs[:-1], EARLY_SPOTS, refs[-1], half)
+    total = place_pieces(order, step, refs[:-2], EARLY_SPOTS, refs[-2], half)
+    refs[-1][...] = total
 
 
 def place_early(step, order, pieces, half, full):
     cols = pieces[0].shape[1]
     return pl.pallas_call(
         functools.partial(place_body, step, half),
-        out_shape=jax.ShapeDtypeStruct((full, cols), jnp.bfloat16),
+        out_shape=[
+            jax.ShapeDtypeStruct((full, cols), jnp.bfloat16),
+            jax.ShapeDtypeStruct((8, cols), jnp.float32),
+        ],
         in_specs=[smem()] + [vmem()] * len(pieces),
-        out_specs=vmem(),
+        out_specs=[vmem()] * 2,
         name="place_early",
         compiler_params=pltpu.CompilerParams(vmem_limit_bytes=14 * 2**20),
         cost_estimate=pl.CostEstimate(
@@ -228,25 +241,17 @@
 def first_body(step, n_right, n_left, order, *refs):
     right = refs[:n_right]
     left = refs[n_right : n_right + n_left]
-    top, bottom, panel, wide, summed = refs[n_right + n_left + 1 :]
-    rows, cols = summed.shape
+    top, bottom, panel, wide, summed = refs[n_right + n_left + 2 :]
+    earlier = refs[n_right + n_left + 1]
+    rows, _ = summed.shape
     half = rows // 2
-    place_pieces(order, step, right, LATE_SPOTS, panel, half)
+    total = place_pieces(order, step, right, LATE_SPOTS, panel, half)
     lay_rows(order, left, wide, 0, rows)
     multiply(wide, panel, summed)
     top[:half, :] = summed[:half, :].astype(jnp.bfloat16)
     bottom[...] = summed[half:, :].astype(jnp.bfloat16)
     if step == 0:
-        block = 128
-
-        def add(k, total):
-            start = pl.multiple_of(k * block, block)
-            part = panel[pl.ds(start, block), :].astype(jnp.float32)
-            return total + fold_rows(part * part)
-
-        total = jnp.zeros((8, cols), jnp.float32)
-        total = lax.fori_loop(0, panel.shape[0] // block, add, total)
-        write_parts(fold_lanes(total), top, half)
+        write_parts(fold_lanes(total + earlier[...]), top, half)
 
 
 def first_product(step, order, right, left, rows, cols):
@@ -258,12 +263,12 @@
         jax.ShapeDtypeStruct((half, cols), jnp.bfloat16),
         jax.ShapeDtypeStruct((full, cols), jnp.bfloat16),
     ]
-    started = place_early(step, order, [right[k] for k in EARLY], half, full)
+    started, total = place_early(step, order, [right[k] for k in EARLY], half, full)
     right = [right[k] for k in LATE]
     return pl.pallas_call(
         functools.partial(first_body, step, len(right), len(left)),
         out_shape=shapes,
-        in_specs=[smem()] + [vmem()] * (len(right) + len(left) + 1),
+        in_specs=[smem()] + [vmem()] * (len(right) + len(left) + 2),
         input_output_aliases={1 + len(right) + len(left): 2},
         out_specs=[vmem()] * len(shapes),
         scratch_shapes=[
@@ -275,7 +280,7 @@
         cost_estimate=pl.CostEstimate(
             flops=2 * rows * cols * full, bytes_accessed=2 * full * cols, transcendentals=0
         ),
-    )(order, *right, *left, started)
+    )(order, *right, *left, started, total)
 
 
 def second_body(step, part, order, shift, panel, current, *refs):

time: 219 us -> 218 us (level)
  no operation moved by 1% of the time
where the time goes in v3:
time: 218 us; the launch traced here: 215 us
  waiting for transfers between devices  104 us (48%)
  starting transfers between devices  81.9 us (38%)
  Pallas kernels  18.5 us (8%)
  local copies, waits for them, and re-layouts  8.84 us (4%)
    ppermute x56, waiting for transfers between devices, permute(): lax.ppermute(value, AXES, [(rank(*d), rank(*target(*d))) for d in EVERY])  104 us
    ppermute x56, starting transfers between devices, permute(): lax.ppermute(value, AXES, [(rank(*d), rank(*target(*d))) for d in EVERY])  81.9 us
    pallas_call x4, Pallas kernels, second_product(): pl.pallas_call(functools.partial(second_body, step, part), out_shape=shap...  9.84 us
    pallas_call x2, Pallas kernels, first_product(): pl.pallas_call(functools.partial(first_body, step, len(right), len(left))...  6.51 us
    unnamed x22, local copies, waits for them, and re-layouts  6.28 us
  transfers between devices with their start and end apart: 56, of which 36 were waited for; matrix products, arithmetic and copies ran while one was open for 4% of the time, Pallas kernels for 4%

profile of v3, /device:TPU:32, one launch (start us, length us, event | category | flops | bytes accessed | tf_op | source)
XLA Modules:
  0.0 214.9 jit_solution(1852681177862030081)
XLA Ops:
  5.9 2.6 %collective-permute-start.2 = (bf16[160,640]{1,0:T(8,128)(2,1)S(1)}, bf16[160,640]{1,0:T(8,128)(2,1)S(1)}, u32[]{:S(2)}, u32[]{:S(2)}) collective-permute-start(bf16[160,640]{1,0:T(8,128)(2,1)S(1)} %pad_maximum_fusion.4), channel_id=1, source_target_pairs={{0,200},{1,201},{2,202},{3,203},{4,204},{5,205},{6,206},{7,207},{8... | collective-permute-start | bytes 614408 | tf_op jit(solution)/shard_map/ppermute | solution.py:36
  9.4 2.9 %collective-permute-done.2 = bf16[160,640]{1,0:T(8,128)(2,1)S(1)} collective-permute-done((bf16[160,640]{1,0:T(8,128)(2,1)S(1)}, bf16[160,640]{1,0:T(8,128)(2,1)S(1)}, u32[]{:S(2)}, u32[]{:S(2)}) %collective-permute-start.2) | collective-permute-done | bytes 204832 | tf_op jit(solution)/shard_map/ppermute | solution.py:36
  29.6 3.6 %collective-permute-done.11 = bf16[160,640]{1,0:T(8,128)(2,1)S(1)} collective-permute-done((bf16[160,640]{1,0:T(8,128)(2,1)S(1)}, bf16[160,640]{1,0:T(8,128)(2,1)S(1)}, u32[]{:S(2)}, u32[]{:S(2)}) %collective-permute-start.11) | collective-permute-done | bytes 204832 | tf_op jit(solution)/shard_map/ppermute | solution.py:36
  33.3 4.3 %collective-permute-start.12 = (bf16[320,640]{1,0:T(8,128)(2,1)S(1)}, bf16[320,640]{1,0:T(8,128)(2,1)S(1)}, u32[]{:S(2)}, u32[]{:S(2)}) collective-permute-start(bf16[320,640]{1,0:T(8,128)(2,1)S(1)} %constant_dynamic-update-slice_fusion.8.refs_4_), channel_id=1, source_target_pairs={{0,15},{1,8},{2,9},{3,10},{4,11},{5,12},{6,13},{7,14},{8,1},{9,2},... | collective-permute-start | bytes 1228808 | tf_op jit(solution)/shard_map/ppermute | solution.py:36
  37.6 5.6 %collective-permute-done.12.refs_5_ = bf16[320,640]{1,0:T(8,128)(2,1)S(1)} collective-permute-done((bf16[320,640]{1,0:T(8,128)(2,1)S(1)}, bf16[320,640]{1,0:T(8,128)(2,1)S(1)}, u32[]{:S(2)}, u32[]{:S(2)}) %collective-permute-start.12) | collective-permute-done | bytes 409632 | tf_op jit(solution)/shard_map/ppermute | solution.py:36
  45.1 5.5 %collective-permute-done.13.refs_6_ = bf16[320,640]{1,0:T(8,128)(2,1)S(1)} collective-permute-done((bf16[320,640]{1,0:T(8,128)(2,1)S(1)}, bf16[320,640]{1,0:T(8,128)(2,1)S(1)}, u32[]{:S(2)}, u32[]{:S(2)}) %collective-permute-start.13) | collective-permute-done | bytes 409632 | tf_op jit(solution)/shard_map/ppermute | solution.py:36
  50.6 3.0 %collective-permute-start.14 = (bf16[320,640]{1,0:T(8,128)(2,1)S(1)}, bf16[320,640]{1,0:T(8,128)(2,1)S(1)}, u32[]{:S(2)}, u32[]{:S(2)}) collective-permute-start(bf16[320,640]{1,0:T(8,128)(2,1)S(1)} %collective-permute-done.13.refs_6_), channel_id=1, source_target_pairs={{0,15},{1,8},{2,9},{3,10},{4,11},{5,12},{6,13},{7,14},{8,1},{9,2},... | collective-permute-start | bytes 1228808 | tf_op jit(solution)/shard_map/ppermute | solution.py:36
  54.7 4.5 %collective-permute-done.14.refs_7_ = bf16[320,640]{1,0:T(8,128)(2,1)S(1)} collective-permute-done((bf16[320,640]{1,0:T(8,128)(2,1)S(1)}, bf16[320,640]{1,0:T(8,128)(2,1)S(1)}, u32[]{:S(2)}, u32[]{:S(2)}) %collective-permute-start.14) | collective-permute-done | bytes 409632 | tf_op jit(solution)/shard_map/ppermute | solution.py:36
  59.2 3.3 %first_product.2 = (bf16[96,640]{1,0:T(8,128)(2,1)S(1)}, bf16[80,640]{1,0:T(8,128)(2,1)S(1)}, bf16[5120,640]{1,0:T(8,128)(2,1)S(1)}) custom-call(s32[136]{0:T(256)S(1)} %bitcast.3, bf16[640,640]{1,0:T(8,128)(2,1)S(1)} %collective-permute-done.4.refs_0_, bf16[640,640]{1,0:T(8,128)(2,1)S(1)} %collective-permute-done.8.refs_1_, ...), custom_call_target="tpu_custom_call", output_to_operand_aliasing={{2}: (9, {})} | custom-call | flops 1048576000 | bytes 6553600 | tf_op jit(solution)/shard_map/first_product/pallas_call | solution.py:268
  66.9 3.0 %collective-permute-start.17 = (bf16[192,640]{1,0:T(8,128)(2,1)S(1)}, bf16[192,640]{1,0:T(8,128)(2,1)S(1)}, u32[]{:S(2)}, u32[]{:S(2)}) collective-permute-start(bf16[192,640]{1,0:T(8,128)(2,1)S(1)} %constant_dynamic-update-slice_fusion.18.refs_0_), channel_id=1, source_target_pairs={{0,15},{1,8},{2,9},{3,10},{4,11},{5,12},{6,13},{7,14},{8,1},{9,2},... | collective-permute-start | bytes 737288 | tf_op jit(solution)/shard_map/ppermute | solution.py:36
  70.0 2.6 %collective-permute-start.25 = (bf16[160,640]{1,0:T(8,128)(2,1)S(1)}, bf16[160,640]{1,0:T(8,128)(2,1)S(1)}, u32[]{:S(2)}, u32[]{:S(2)}) collective-permute-start(bf16[160,640]{1,0:T(8,128)(2,1)S(1)} %constant_dynamic-update-slice_fusion.24.refs_0_), channel_id=1, source_target_pairs={{0,15},{1,8},{2,9},{3,10},{4,11},{5,12},{6,13},{7,14},{8,1},{9,2},... | collective-permute-start | bytes 614408 | tf_op jit(solution)/shard_map/ppermute | solution.py:36
  79.5 3.1 %collective-permute-start.19 = (bf16[192,640]{1,0:T(8,128)(2,1)S(1)}, bf16[192,640]{1,0:T(8,128)(2,1)S(1)}, u32[]{:S(2)}, u32[]{:S(2)}) collective-permute-start(bf16[192,640]{1,0:T(8,128)(2,1)S(1)} %collective-permute-done.18.refs_2_), channel_id=1, source_target_pairs={{0,15},{1,8},{2,9},{3,10},{4,11},{5,12},{6,13},{7,14},{8,1},{9,2},... | collective-permute-start | bytes 737288 | tf_op jit(solution)/shard_map/ppermute | solution.py:36
  102.4 4.5 %collective-permute-start.30 = (bf16[320,640]{1,0:T(8,128)(2,1)S(1)}, bf16[320,640]{1,0:T(8,128)(2,1)S(1)}, u32[]{:S(2)}, u32[]{:S(2)}) collective-permute-start(bf16[320,640]{1,0:T(8,128)(2,1)S(1)} %pad_maximum_fusion.3), channel_id=1, source_target_pairs={{0,56},{1,57},{2,58},{3,59},{4,60},{5,61},{6,62},{7,63},{8,192},{9... | collective-permute-start | bytes 1228808 | tf_op jit(solution)/shard_map/ppermute | solution.py:36
  108.4 4.2 %collective-permute-done.30 = bf16[320,640]{1,0:T(8,128)(2,1)S(1)} collective-permute-done((bf16[320,640]{1,0:T(8,128)(2,1)S(1)}, bf16[320,640]{1,0:T(8,128)(2,1)S(1)}, u32[]{:S(2)}, u32[]{:S(2)}) %collective-permute-start.30) | collective-permute-done | bytes 409632 | tf_op jit(solution)/shard_map/ppermute | solution.py:36
  116.0 5.2 %collective-permute-done.34 = bf16[160,640]{1,0:T(8,128)(2,1)S(1)} collective-permute-done((bf16[160,640]{1,0:T(8,128)(2,1)S(1)}, bf16[160,640]{1,0:T(8,128)(2,1)S(1)}, u32[]{:S(2)}, u32[]{:S(2)}) %collective-permute-start.34) | collective-permute-done | bytes 204832 | tf_op jit(solution)/shard_map/ppermute | solution.py:36
  121.1 3.2 %collective-permute-start.35 = (bf16[320,640]{1,0:T(8,128)(2,1)S(1)}, bf16[320,640]{1,0:T(8,128)(2,1)S(1)}, u32[]{:S(2)}, u32[]{:S(2)}) collective-permute-start(bf16[320,640]{1,0:T(8,128)(2,1)S(1)} %constant_dynamic-update-slice_fusion.30.refs_4_), channel_id=1, source_target_pairs={{0,15},{1,8},{2,9},{3,10},{4,11},{5,12},{6,13},{7,14},{8,1},{9,2},... | collective-permute-start | bytes 1228808 | tf_op jit(solution)/shard_map/ppermute | solution.py:36
  124.3 5.6 %collective-permute-done.35.refs_5_ = bf16[320,640]{1,0:T(8,128)(2,1)S(1)} collective-permute-done((bf16[320,640]{1,0:T(8,128)(2,1)S(1)}, bf16[320,640]{1,0:T(8,128)(2,1)S(1)}, u32[]{:S(2)}, u32[]{:S(2)}) %collective-permute-start.35) | collective-permute-done | bytes 409632 | tf_op jit(solution)/shard_map/ppermute | solution.py:36
  132.3 5.0 %collective-permute-done.36.refs_6_ = bf16[320,640]{1,0:T(8,128)(2,1)S(1)} collective-permute-done((bf16[320,640]{1,0:T(8,128)(2,1)S(1)}, bf16[320,640]{1,0:T(8,128)(2,1)S(1)}, u32[]{:S(2)}, u32[]{:S(2)}) %collective-permute-start.36) | collective-permute-done | bytes 409632 | tf_op jit(solution)/shard_map/ppermute | solution.py:36
  137.3 3.1 %collective-permute-start.37 = (bf16[320,640]{1,0:T(8,128)(2,1)S(1)}, bf16[320,640]{1,0:T(8,128)(2,1)S(1)}, u32[]{:S(2)}, u32[]{:S(2)}) collective-permute-start(bf16[320,640]{1,0:T(8,128)(2,1)S(1)} %collective-permute-done.36.refs_6_), channel_id=1, source_target_pairs={{0,15},{1,8},{2,9},{3,10},{4,11},{5,12},{6,13},{7,14},{8,1},{9,2},... | collective-permute-start | bytes 1228808 | tf_op jit(solution)/shard_map/ppermute | solution.py:36
  141.5 4.6 %collective-permute-done.37.refs_7_ = bf16[320,640]{1,0:T(8,128)(2,1)S(1)} collective-permute-done((bf16[320,640]{1,0:T(8,128)(2,1)S(1)}, bf16[320,640]{1,0:T(8,128)(2,1)S(1)}, u32[]{:S(2)}, u32[]{:S(2)}) %collective-permute-start.37) | collective-permute-done | bytes 409632 | tf_op jit(solution)/shard_map/ppermute | solution.py:36
  146.1 3.2 %first_product.3 = (bf16[80,640]{1,0:T(8,128)(2,1)S(1)}, bf16[80,640]{1,0:T(8,128)(2,1)S(1)}, bf16[5120,640]{1,0:T(8,128)(2,1)S(1)}) custom-call(s32[136]{0:T(256)S(1)} %bitcast.7, bf16[640,640]{1,0:T(8,128)(2,1)S(1)} %collective-permute-done.23.refs_0_, bf16[640,640]{1,0:T(8,128)(2,1)S(1)} %collective-permute-done.31.refs_1_, ...), custom_call_target="tpu_custom_call", output_to_operand_aliasing={{2}: (9, {})} | custom-call | flops 1048576000 | bytes 6553600 | tf_op jit(solution)/shard_map/first_product/pallas_call | solution.py:268
  151.2 3.3 %collective-permute-done.43 = bf16[80,640]{1,0:T(8,128)(2,1)S(1)} collective-permute-done((bf16[80,640]{1,0:T(8,128)(2,1)S(1)}, bf16[80,640]{1,0:T(8,128)(2,1)S(1)}, u32[]{:S(2)}, u32[]{:S(2)}) %collective-permute-start.43) | collective-permute-done | bytes 102432 | tf_op jit(solution)/shard_map/ppermute | solution.py:36
  154.6 4.6 %collective-permute-start.44 = (bf16[160,640]{1,0:T(8,128)(2,1)S(1)}, bf16[160,640]{1,0:T(8,128)(2,1)S(1)}, u32[]{:S(2)}, u32[]{:S(2)}) collective-permute-start(bf16[160,640]{1,0:T(8,128)(2,1)S(1)} %constant_dynamic-update-slice_fusion.42.refs_0_), channel_id=1, source_target_pairs={{0,15},{1,8},{2,9},{3,10},{4,11},{5,12},{6,13},{7,14},{8,1},{9,2},... | collective-permute-start | bytes 614408 | tf_op jit(solution)/shard_map/ppermute | solution.py:36
  159.3 3.3 %collective-permute-done.44.refs_1_ = bf16[160,640]{1,0:T(8,128)(2,1)S(1)} collective-permute-done((bf16[160,640]{1,0:T(8,128)(2,1)S(1)}, bf16[160,640]{1,0:T(8,128)(2,1)S(1)}, u32[]{:S(2)}, u32[]{:S(2)}) %collective-permute-start.44) | collective-permute-done | bytes 204832 | tf_op jit(solution)/shard_map/ppermute | solution.py:36
  163.1 2.6 %collective-permute-done.40.refs_1_ = bf16[160,640]{1,0:T(8,128)(2,1)S(1)} collective-permute-done((bf16[160,640]{1,0:T(8,128)(2,1)S(1)}, bf16[160,640]{1,0:T(8,128)(2,1)S(1)}, u32[]{:S(2)}, u32[]{:S(2)}) %collective-permute-start.40) | collective-permute-done | bytes 204832 | tf_op jit(solution)/shard_map/ppermute | solution.py:36
  167.8 3.2 %collective-permute-start.46 = (bf16[160,640]{1,0:T(8,128)(2,1)S(1)}, bf16[160,640]{1,0:T(8,128)(2,1)S(1)}, u32[]{:S(2)}, u32[]{:S(2)}) collective-permute-start(bf16[160,640]{1,0:T(8,128)(2,1)S(1)} %collective-permute-done.45.refs_2_), channel_id=1, source_target_pairs={{0,15},{1,8},{2,9},{3,10},{4,11},{5,12},{6,13},{7,14},{8,1},{9,2},... | collective-permute-start | bytes 614408 | tf_op jit(solution)/shard_map/ppermute | solution.py:36
  171.3 4.5 %collective-permute-start.42 = (bf16[160,640]{1,0:T(8,128)(2,1)S(1)}, bf16[160,640]{1,0:T(8,128)(2,1)S(1)}, u32[]{:S(2)}, u32[]{:S(2)}) collective-permute-start(bf16[160,640]{1,0:T(8,128)(2,1)S(1)} %collective-permute-done.41.refs_2_), channel_id=1, source_target_pairs={{0,15},{1,8},{2,9},{3,10},{4,11},{5,12},{6,13},{7,14},{8,1},{9,2},... | collective-permute-start | bytes 614408 | tf_op jit(solution)/shard_map/ppermute | solution.py:36
  186.7 4.4 %collective-permute-done.50 = f32[32,128]{1,0:T(8,128)S(1)} collective-permute-done((f32[32,128]{1,0:T(8,128)S(1)}, f32[32,128]{1,0:T(8,128)S(1)}, u32[]{:S(2)}, u32[]{:S(2)}) %collective-permute-start.50) | collective-permute-done | bytes 16416 | tf_op jit(solution)/shard_map/ppermute | solution.py:36
  191.1 3.2 %collective-permute-done.51 = f32[32,128]{1,0:T(8,128)S(1)} collective-permute-done((f32[32,128]{1,0:T(8,128)S(1)}, f32[32,128]{1,0:T(8,128)S(1)}, u32[]{:S(2)}, u32[]{:S(2)}) %collective-permute-start.51) | collective-permute-done | bytes 16416 | tf_op jit(solution)/shard_map/ppermute | solution.py:36
  194.2 4.4 %collective-permute-done.52 = f32[32,128]{1,0:T(8,128)S(1)} collective-permute-done((f32[32,128]{1,0:T(8,128)S(1)}, f32[32,128]{1,0:T(8,128)S(1)}, u32[]{:S(2)}, u32[]{:S(2)}) %collective-permute-start.52) | collective-permute-done | bytes 16416 | tf_op jit(solution)/shard_map/ppermute | solution.py:36
  201.8 4.1 %collective-permute-done.54 = f32[32,128]{1,0:T(8,128)S(1)} collective-permute-done((f32[32,128]{1,0:T(8,128)S(1)}, f32[32,128]{1,0:T(8,128)S(1)}, u32[]{:S(2)}, u32[]{:S(2)}) %collective-permute-start.54) | collective-permute-done | bytes 16416 | tf_op jit(solution)/shard_map/ppermute | solution.py:36
  208.2 4.9 %collective-permute-done.55 = f32[32,128]{1,0:T(8,128)S(1)} collective-permute-done((f32[32,128]{1,0:T(8,128)S(1)}, f32[32,128]{1,0:T(8,128)S(1)}, u32[]{:S(2)}, u32[]{:S(2)}) %collective-permute-start.55) | collective-permute-done | bytes 16416 | tf_op jit(solution)/shard_map/ppermute | solution.py:36
  (141 shorter events, 89.0 us)
Async XLA Ops:
  5.1 22.9 %collective-permute-start = (bf16[160,640]{1,0:T(8,128)(2,1)S(1)}, bf16[160,640]{1,0:T(8,128)(2,1)S(1)}, u32[]{:S(2)}, u32[]{:S(2)}) collective-permute-start(bf16[160,640]{1,0:T(8,128)(2,1)S(1)} %get-tuple-element.31), channel_id=1, source_target_pairs={{0,8},{1,9},{2,10},{3,11},{4,12},{5,13},{6,14},{7,15},{8,0},{9,1},... | collective-permute-start | bytes 614408 | tf_op jit(solution)/shard_map/ppermute | solution.py:36
  12.4 7.5 %collective-permute-start.3 = (bf16[320,640]{1,0:T(8,128)(2,1)S(1)}, bf16[320,640]{1,0:T(8,128)(2,1)S(1)}, u32[]{:S(2)}, u32[]{:S(2)}) collective-permute-start(bf16[320,640]{1,0:T(8,128)(2,1)S(1)} %pad_maximum_fusion), channel_id=1, source_target_pairs={{0,24},{1,25},{2,26},{3,27},{4,28},{5,29},{6,30},{7,31},{8,64},{9,... | collective-permute-start | bytes 1228808 | tf_op jit(solution)/shard_map/ppermute | solution.py:36
  15.2 8.7 %collective-permute-start.7 = (bf16[320,640]{1,0:T(8,128)(2,1)S(1)}, bf16[320,640]{1,0:T(8,128)(2,1)S(1)}, u32[]{:S(2)}, u32[]{:S(2)}) collective-permute-start(bf16[320,640]{1,0:T(8,128)(2,1)S(1)} %pad_maximum_fusion.1), channel_id=1, source_target_pairs={{0,56},{1,57},{2,58},{3,59},{4,60},{5,61},{6,62},{7,63},{8,192},{9... | collective-permute-start | bytes 1228808 | tf_op jit(solution)/shard_map/ppermute | solution.py:36
  24.7 19.0 %collective-permute-start.8 = (bf16[640,640]{1,0:T(8,128)(2,1)S(1)}, bf16[640,640]{1,0:T(8,128)(2,1)S(1)}, u32[]{:S(2)}, u32[]{:S(2)}) collective-permute-start(bf16[640,640]{1,0:T(8,128)(2,1)S(1)} %get-tuple-element.66.refs_1_), channel_id=1, source_target_pairs={{0,24},{1,25},{2,26},{3,27},{4,28},{5,29},{6,30},{7,31},{8,64},{9,... | collective-permute-start | bytes 2457608 | tf_op jit(solution)/shard_map/ppermute | solution.py:36
  25.3 19.7 %collective-permute-start.4 = (bf16[640,640]{1,0:T(8,128)(2,1)S(1)}, bf16[640,640]{1,0:T(8,128)(2,1)S(1)}, u32[]{:S(2)}, u32[]{:S(2)}) collective-permute-start(bf16[640,640]{1,0:T(8,128)(2,1)S(1)} %get-tuple-element.68.refs_0_), channel_id=1, source_target_pairs={{0,56},{1,57},{2,58},{3,59},{4,60},{5,61},{6,62},{7,63},{8,192},{9... | collective-permute-start | bytes 2457608 | tf_op jit(solution)/shard_map/ppermute | solution.py:36
  27.2 26.3 %collective-permute-start.15 = (bf16[1280,640]{1,0:T(8,128)(2,1)}, bf16[1280,640]{1,0:T(8,128)(2,1)S(1)}, u32[]{:S(2)}, u32[]{:S(2)}) collective-permute-start(bf16[1280,640]{1,0:T(8,128)(2,1)} %get-tuple-element.65), channel_id=1, source_target_pairs={{0,8},{1,9},{2,10},{3,11},{4,12},{5,13},{6,14},{7,15},{8,0},{9,1},... | collective-permute-start | bytes 4915208 | tf_op jit(solution)/shard_map/ppermute | solution.py:36
  33.3 10.0 %collective-permute-start.12 = (bf16[320,640]{1,0:T(8,128)(2,1)S(1)}, bf16[320,640]{1,0:T(8,128)(2,1)S(1)}, u32[]{:S(2)}, u32[]{:S(2)}) collective-permute-start(bf16[320,640]{1,0:T(8,128)(2,1)S(1)} %constant_dynamic-update-slice_fusion.8.refs_4_), channel_id=1, source_target_pairs={{0,15},{1,8},{2,9},{3,10},{4,11},{5,12},{6,13},{7,14},{8,1},{9,2},... | collective-permute-start | bytes 1228808 | tf_op jit(solution)/shard_map/ppermute | solution.py:36
  43.2 7.4 %collective-permute-start.13 = (bf16[320,640]{1,0:T(8,128)(2,1)S(1)}, bf16[320,640]{1,0:T(8,128)(2,1)S(1)}, u32[]{:S(2)}, u32[]{:S(2)}) collective-permute-start(bf16[320,640]{1,0:T(8,128)(2,1)S(1)} %collective-permute-done.12.refs_5_), channel_id=1, source_target_pairs={{0,9},{1,10},{2,11},{3,12},{4,13},{5,14},{6,15},{7,8},{8,7},{9,0},... | collective-permute-start | bytes 1228808 | tf_op jit(solution)/shard_map/ppermute | solution.py:36
  43.8 15.4 %collective-permute-start.10 = (bf16[640,640]{1,0:T(8,128)(2,1)S(1)}, bf16[640,640]{1,0:T(8,128)(2,1)S(1)}, u32[]{:S(2)}, u32[]{:S(2)}) collective-permute-start(bf16[640,640]{1,0:T(8,128)(2,1)S(1)} %collective-permute-done.8.refs_1_), channel_id=1, source_target_pairs={{0,8},{1,9},{2,10},{3,11},{4,12},{5,13},{6,14},{7,15},{8,0},{9,1},... | collective-permute-start | bytes 2457608 | tf_op jit(solution)/shard_map/ppermute | solution.py:36
  45.0 14.2 %collective-permute-start.9 = (bf16[640,640]{1,0:T(8,128)(2,1)S(1)}, bf16[640,640]{1,0:T(8,128)(2,1)S(1)}, u32[]{:S(2)}, u32[]{:S(2)}) collective-permute-start(bf16[640,640]{1,0:T(8,128)(2,1)S(1)} %collective-permute-done.4.refs_0_), channel_id=1, source_target_pairs={{0,8},{1,9},{2,10},{3,11},{4,12},{5,13},{6,14},{7,15},{8,0},{9,1},... | collective-permute-start | bytes 2457608 | tf_op jit(solution)/shard_map/ppermute | solution.py:36
  50.6 8.6 %collective-permute-start.14 = (bf16[320,640]{1,0:T(8,128)(2,1)S(1)}, bf16[320,640]{1,0:T(8,128)(2,1)S(1)}, u32[]{:S(2)}, u32[]{:S(2)}) collective-permute-start(bf16[320,640]{1,0:T(8,128)(2,1)S(1)} %collective-permute-done.13.refs_6_), channel_id=1, source_target_pairs={{0,15},{1,8},{2,9},{3,10},{4,11},{5,12},{6,13},{7,14},{8,1},{9,2},... | collective-permute-start | bytes 1228808 | tf_op jit(solution)/shard_map/ppermute | solution.py:36
  63.2 6.8 %collective-permute-start.24 = (bf16[80,640]{1,0:T(8,128)(2,1)S(1)}, bf16[80,640]{1,0:T(8,128)(2,1)S(1)}, u32[]{:S(2)}, u32[]{:S(2)}) collective-permute-start(bf16[80,640]{1,0:T(8,128)(2,1)S(1)} %get-tuple-element.42), channel_id=1, source_target_pairs={{0,9},{1,10},{2,11},{3,12},{4,13},{5,14},{6,15},{7,8},{8,7},{9,0},... | collective-permute-start | bytes 307208 | tf_op jit(solution)/shard_map/ppermute | solution.py:36
  66.9 6.9 %collective-permute-start.17 = (bf16[192,640]{1,0:T(8,128)(2,1)S(1)}, bf16[192,640]{1,0:T(8,128)(2,1)S(1)}, u32[]{:S(2)}, u32[]{:S(2)}) collective-permute-start(bf16[192,640]{1,0:T(8,128)(2,1)S(1)} %constant_dynamic-update-slice_fusion.18.refs_0_), channel_id=1, source_target_pairs={{0,15},{1,8},{2,9},{3,10},{4,11},{5,12},{6,13},{7,14},{8,1},{9,2},... | collective-permute-start | bytes 737288 | tf_op jit(solution)/shard_map/ppermute | solution.py:36
  76.0 6.6 %collective-permute-start.26 = (bf16[160,640]{1,0:T(8,128)(2,1)S(1)}, bf16[160,640]{1,0:T(8,128)(2,1)S(1)}, u32[]{:S(2)}, u32[]{:S(2)}) collective-permute-start(bf16[160,640]{1,0:T(8,128)(2,1)S(1)} %collective-permute-done.25.refs_1_), channel_id=1, source_target_pairs={{0,9},{1,10},{2,11},{3,12},{4,13},{5,14},{6,15},{7,8},{8,7},{9,0},... | collective-permute-start | bytes 614408 | tf_op jit(solution)/shard_map/ppermute | solution.py:36
  79.5 7.0 %collective-permute-start.19 = (bf16[192,640]{1,0:T(8,128)(2,1)S(1)}, bf16[192,640]{1,0:T(8,128)(2,1)S(1)}, u32[]{:S(2)}, u32[]{:S(2)}) collective-permute-start(bf16[192,640]{1,0:T(8,128)(2,1)S(1)} %collective-permute-done.18.refs_2_), channel_id=1, source_target_pairs={{0,15},{1,8},{2,9},{3,10},{4,11},{5,12},{6,13},{7,14},{8,1},{9,2},... | collective-permute-start | bytes 737288 | tf_op jit(solution)/shard_map/ppermute | solution.py:36
  82.6 6.6 %collective-permute-start.27 = (bf16[160,640]{1,0:T(8,128)(2,1)S(1)}, bf16[160,640]{1,0:T(8,128)(2,1)S(1)}, u32[]{:S(2)}, u32[]{:S(2)}) collective-permute-start(bf16[160,640]{1,0:T(8,128)(2,1)S(1)} %collective-permute-done.26.refs_2_), channel_id=1, source_target_pairs={{0,15},{1,8},{2,9},{3,10},{4,11},{5,12},{6,13},{7,14},{8,1},{9,2},... | collective-permute-start | bytes 614408 | tf_op jit(solution)/shard_map/ppermute | solution.py:36
  99.9 8.2 %collective-permute-start.22 = (bf16[320,640]{1,0:T(8,128)(2,1)S(1)}, bf16[320,640]{1,0:T(8,128)(2,1)S(1)}, u32[]{:S(2)}, u32[]{:S(2)}) collective-permute-start(bf16[320,640]{1,0:T(8,128)(2,1)S(1)} %pad_maximum_fusion.2), channel_id=1, source_target_pairs={{0,24},{1,25},{2,26},{3,27},{4,28},{5,29},{6,30},{7,31},{8,64},{9,... | collective-permute-start | bytes 1228808 | tf_op jit(solution)/shard_map/ppermute | solution.py:36
  102.4 10.2 %collective-permute-start.30 = (bf16[320,640]{1,0:T(8,128)(2,1)S(1)}, bf16[320,640]{1,0:T(8,128)(2,1)S(1)}, u32[]{:S(2)}, u32[]{:S(2)}) collective-permute-start(bf16[320,640]{1,0:T(8,128)(2,1)S(1)} %pad_maximum_fusion.3), channel_id=1, source_target_pairs={{0,56},{1,57},{2,58},{3,59},{4,60},{5,61},{6,62},{7,63},{8,192},{9... | collective-permute-start | bytes 1228808 | tf_op jit(solution)/shard_map/ppermute | solution.py:36
  112.7 27.8 %collective-permute-start.38 = (bf16[1280,640]{1,0:T(8,128)(2,1)S(1)}, bf16[1280,640]{1,0:T(8,128)(2,1)S(1)}, u32[]{:S(2)}, u32[]{:S(2)}) collective-permute-start(bf16[1280,640]{1,0:T(8,128)(2,1)S(1)} %get-tuple-element.61), channel_id=1, source_target_pairs={{0,8},{1,9},{2,10},{3,11},{4,12},{5,13},{6,14},{7,15},{8,0},{9,1},... | collective-permute-start | bytes 4915208 | tf_op jit(solution)/shard_map/ppermute | solution.py:36
  113.5 17.1 %collective-permute-start.31 = (bf16[640,640]{1,0:T(8,128)(2,1)S(1)}, bf16[640,640]{1,0:T(8,128)(2,1)S(1)}, u32[]{:S(2)}, u32[]{:S(2)}) collective-permute-start(bf16[640,640]{1,0:T(8,128)(2,1)S(1)} %get-tuple-element.62.refs_1_), channel_id=1, source_target_pairs={{0,24},{1,25},{2,26},{3,27},{4,28},{5,29},{6,30},{7,31},{8,64},{9,... | collective-permute-start | bytes 2457608 | tf_op jit(solution)/shard_map/ppermute | solution.py:36
  113.5 18.8 %collective-permute-start.23 = (bf16[640,640]{1,0:T(8,128)(2,1)S(1)}, bf16[640,640]{1,0:T(8,128)(2,1)S(1)}, u32[]{:S(2)}, u32[]{:S(2)}) collective-permute-start(bf16[640,640]{1,0:T(8,128)(2,1)S(1)} %get-tuple-element.64.refs_0_), channel_id=1, source_target_pairs={{0,56},{1,57},{2,58},{3,59},{4,60},{5,61},{6,62},{7,63},{8,192},{9... | collective-permute-start | bytes 2457608 | tf_op jit(solution)/shard_map/ppermute | solution.py:36
  121.1 8.8 %collective-permute-start.35 = (bf16[320,640]{1,0:T(8,128)(2,1)S(1)}, bf16[320,640]{1,0:T(8,128)(2,1)S(1)}, u32[]{:S(2)}, u32[]{:S(2)}) collective-permute-start(bf16[320,640]{1,0:T(8,128)(2,1)S(1)} %constant_dynamic-update-slice_fusion.30.refs_4_), channel_id=1, source_target_pairs={{0,15},{1,8},{2,9},{3,10},{4,11},{5,12},{6,13},{7,14},{8,1},{9,2},... | collective-permute-start | bytes 1228808 | tf_op jit(solution)/shard_map/ppermute | solution.py:36
  130.0 7.4 %collective-permute-start.36 = (bf16[320,640]{1,0:T(8,128)(2,1)S(1)}, bf16[320,640]{1,0:T(8,128)(2,1)S(1)}, u32[]{:S(2)}, u32[]{:S(2)}) collective-permute-start(bf16[320,640]{1,0:T(8,128)(2,1)S(1)} %collective-permute-done.35.refs_5_), channel_id=1, source_target_pairs={{0,9},{1,10},{2,11},{3,12},{4,13},{5,14},{6,15},{7,8},{8,7},{9,0},... | collective-permute-start | bytes 1228808 | tf_op jit(solution)/shard_map/ppermute | solution.py:36
  130.6 15.5 %collective-permute-start.33 = (bf16[640,640]{1,0:T(8,128)(2,1)S(1)}, bf16[640,640]{1,0:T(8,128)(2,1)S(1)}, u32[]{:S(2)}, u32[]{:S(2)}) collective-permute-start(bf16[640,640]{1,0:T(8,128)(2,1)S(1)} %collective-permute-done.31.refs_1_), channel_id=1, source_target_pairs={{0,8},{1,9},{2,10},{3,11},{4,12},{5,13},{6,14},{7,15},{8,0},{9,1},... | collective-permute-start | bytes 2457608 | tf_op jit(solution)/shard_map/ppermute | solution.py:36
  132.3 13.8 %collective-permute-start.32 = (bf16[640,640]{1,0:T(8,128)(2,1)S(1)}, bf16[640,640]{1,0:T(8,128)(2,1)S(1)}, u32[]{:S(2)}, u32[]{:S(2)}) collective-permute-start(bf16[640,640]{1,0:T(8,128)(2,1)S(1)} %collective-permute-done.23.refs_0_), channel_id=1, source_target_pairs={{0,8},{1,9},{2,10},{3,11},{4,12},{5,13},{6,14},{7,15},{8,0},{9,1},... | collective-permute-start | bytes 2457608 | tf_op jit(solution)/shard_map/ppermute | solution.py:36
  137.3 8.7 %collective-permute-start.37 = (bf16[320,640]{1,0:T(8,128)(2,1)S(1)}, bf16[320,640]{1,0:T(8,128)(2,1)S(1)}, u32[]{:S(2)}, u32[]{:S(2)}) collective-permute-start(bf16[320,640]{1,0:T(8,128)(2,1)S(1)} %collective-permute-done.36.refs_6_), channel_id=1, source_target_pairs={{0,15},{1,8},{2,9},{3,10},{4,11},{5,12},{6,13},{7,14},{8,1},{9,2},... | collective-permute-start | bytes 1228808 | tf_op jit(solution)/shard_map/ppermute | solution.py:36
  149.3 9.8 %collective-permute-start.39 = (bf16[80,640]{1,0:T(8,128)(2,1)S(1)}, bf16[80,640]{1,0:T(8,128)(2,1)S(1)}, u32[]{:S(2)}, u32[]{:S(2)}) collective-permute-start(bf16[80,640]{1,0:T(8,128)(2,1)S(1)} %get-tuple-element.51), channel_id=1, source_target_pairs={{0,9},{1,10},{2,11},{3,12},{4,13},{5,14},{6,15},{7,8},{8,7},{9,0},... | collective-permute-start | bytes 307208 | tf_op jit(solution)/shard_map/ppermute | solution.py:36
  154.6 8.0 %collective-permute-start.44 = (bf16[160,640]{1,0:T(8,128)(2,1)S(1)}, bf16[160,640]{1,0:T(8,128)(2,1)S(1)}, u32[]{:S(2)}, u32[]{:S(2)}) collective-permute-start(bf16[160,640]{1,0:T(8,128)(2,1)S(1)} %constant_dynamic-update-slice_fusion.42.refs_0_), channel_id=1, source_target_pairs={{0,15},{1,8},{2,9},{3,10},{4,11},{5,12},{6,13},{7,14},{8,1},{9,2},... | collective-permute-start | bytes 614408 | tf_op jit(solution)/shard_map/ppermute | solution.py:36
  167.8 8.0 %collective-permute-start.46 = (bf16[160,640]{1,0:T(8,128)(2,1)S(1)}, bf16[160,640]{1,0:T(8,128)(2,1)S(1)}, u32[]{:S(2)}, u32[]{:S(2)}) collective-permute-start(bf16[160,640]{1,0:T(8,128)(2,1)S(1)} %collective-permute-done.45.refs_2_), channel_id=1, source_target_pairs={{0,15},{1,8},{2,9},{3,10},{4,11},{5,12},{6,13},{7,14},{8,1},{9,2},... | collective-permute-start | bytes 614408 | tf_op jit(solution)/shard_map/ppermute | solution.py:36
  171.3 7.9 %collective-permute-start.42 = (bf16[160,640]{1,0:T(8,128)(2,1)S(1)}, bf16[160,640]{1,0:T(8,128)(2,1)S(1)}, u32[]{:S(2)}, u32[]{:S(2)}) collective-permute-start(bf16[160,640]{1,0:T(8,128)(2,1)S(1)} %collective-permute-done.41.refs_2_), channel_id=1, source_target_pairs={{0,15},{1,8},{2,9},{3,10},{4,11},{5,12},{6,13},{7,14},{8,1},{9,2},... | collective-permute-start | bytes 614408 | tf_op jit(solution)/shard_map/ppermute | solution.py:36
  181.7 32.5 %collective-permute-start.47 = (f32[160,640]{1,0:T(8,128)S(1)}, f32[160,640]{1,0:T(8,128)S(1)}, u32[]{:S(2)}, u32[]{:S(2)}) collective-permute-start(f32[160,640]{1,0:T(8,128)S(1)} %get-tuple-element.57), channel_id=1, source_target_pairs={{0,8},{1,9},{2,10},{3,11},{4,12},{5,13},{6,14},{7,15},{8,0},{9,1},... | collective-permute-start | bytes 1228808 | tf_op jit(solution)/shard_map/ppermute | solution.py:36
  205.9 7.2 %collective-permute-start.55 = (f32[32,128]{1,0:T(8,128)S(1)}, f32[32,128]{1,0:T(8,128)S(1)}, u32[]{:S(2)}, u32[]{:S(2)}) collective-permute-start(f32[32,128]{1,0:T(8,128)S(1)} %add.61), channel_id=1, source_target_pairs={{0,12},{1,13},{2,14},{3,15},{4,8},{5,9},{6,10},{7,11},{8,4},{9,5},... | collective-permute-start | bytes 49160 | tf_op jit(solution)/shard_map/ppermute | solution.py:36
  (25 other events, 118.3 us)
